TPU v7x, 128 devices: a whole 4x4x4 slice. The times are simulated.
128 devices in a mesh: section: 8 (over y_hi, x), seq: 16 (over z, y_lo, core).
Axes of the slice: x: 4, y: 4 (y_hi: 2, y_lo: 2; y = y_hi * 2 + y_lo), z: 4, core: 2. Of those that a mesh axis runs over, the one named last changes fastest.
Arguments:
- tokens: bfloat16 [8, 4096, 4096], P('section', 'seq'), may hold values from -6 to 6
- norm_gain: bfloat16 [8, 4096], P('section'), may hold values from 0.099609375 to 1.8984375
- w_query: bfloat16 [8, 4096, 2048], P('section', 'seq'), may hold values from -0.09375 to 0.09375
- w_key: bfloat16 [8, 4096, 512], P('section', 'seq'), may hold values from -1.903125 to 1.903125
- w_value: bfloat16 [8, 4096, 512], P('section', 'seq'), may hold values from -0.09375 to 0.09375
Outputs:
- received: bfloat16 [8, 4096, 2048], P('section', 'seq')
All inputs are finite; a program needn't handle non-finite values.
Results may differ from a plain program's by a relative error of at most 0.012.
The roundings to bfloat16 on the way count: a program that leaves them out, or rounds other values in their place, can miss the bound.
Values may be sent and summed in bfloat16 or wider, within the bound.
No kernel may reach another device: no remote copies, remote signals or barrier semaphores. Data moves between devices by JAX's collectives and lax.ppermute only.
A program may use at most 192 MiB of HBM per device.

v0:
```python
import math

import jax
import jax.numpy as jnp
from jax import lax
from jax.experimental import pallas as pl
from jax.experimental.pallas import tpu as pltpu
from jax.sharding import PartitionSpec as P


HEAD = 128
GROUP = 4
RING = 4
LOG2E_SCALE = math.log2(math.e) / math.sqrt(HEAD)
NEG = -1e30
PROJECT_VMEM = 10 << 20


def near(block, bits):
    return lax.ppermute(block, "seq", [(r, r ^ bits) for r in range(RING * GROUP)])


def along(block, step):
    n = RING * GROUP
    return lax.ppermute(block, "seq", [(r, (r + step * GROUP) % n) for r in range(n)])


def upward(block, routes):
    return lax.ppermute(block, "seq", [(a * GROUP + g, b * GROUP + g) for a, b in routes for g in range(GROUP)])


def onward(block, bits):
    n = RING * GROUP
    s = lax.axis_size("section")
    route = [(i * n + r, ((i + 1) % s) * n + (r ^ bits)) for i in range(s) for r in range(n)]
    return lax.ppermute(block, ("section", "seq"), route)


def normalize(rows_in, gain_row):
    wide = rows_in.astype(jnp.float32)
    scale = lax.rsqrt(jnp.mean(wide * wide, axis=-1, keepdims=True) + 1e-05)
    return (wide * scale * gain_row.astype(jnp.float32)).astype(jnp.bfloat16)


def rope_tables(z, g, rows, pieces):
    at = [(z * GROUP + (g ^ j)) * rows + first + jnp.arange(n) for j, first, n in pieces]
    positions = jnp.concatenate(at).astype(jnp.float32)
    half = HEAD // 2
    freqs = jnp.power(jnp.float32(500000.0), -(jnp.arange(half).astype(jnp.float32) * 2.0 / HEAD))
    angles = positions[:, None] * jnp.concatenate([freqs, freqs])[None, :]
    sign = jnp.where(jnp.arange(HEAD) < half, -1.0, 1.0).astype(jnp.float32)
    return jnp.cos(angles), jnp.sin(angles) * sign[None, :]


def weight_blocks(place_ref, weights, refs, depth):
    z, g = place_ref[0], place_ref[1]
    blocks, at = [], 0
    for off, slab in enumerate(weights):
        j = 0
        for w in slab:
            for row in range(0, w.shape[0], depth):
                start = pl.multiple_of((((z + off) % RING) * GROUP + (g ^ j)) * depth, depth)
                blocks.append((start, refs[at], row))
                j += 1
            at += 1
    return blocks


def turned(x, c, s):
    return (x * c + pltpu.roll(x, HEAD // 2, 1) * s).astype(jnp.bfloat16)


def project(place, chunks, weights, cos_table, sin_table, queries):
    tokens = [t for chunk in chunks for t in chunk]
    rows = sum(t.shape[0] for t in tokens)
    width = tokens[0].shape[1]
    depth = width // (RING * GROUP)
    flat = [w for slab in weights for w in slab]
    tile = 2 * HEAD
    out_width = 2 * tile if queries else tile

    def kernel(place_ref, *refs):
        tok = refs[: len(tokens)]
        wts = refs[len(tokens) : len(tokens) + len(flat)]
        cos_ref, sin_ref, out_ref = refs[len(tokens) + len(flat) :]
        blocks = weight_blocks(place_ref, weights, wts, depth)

        def columns(first_column, out_column):
            at, base = 0, 0
            for chunk in chunks:
                mine = tok[at : at + len(chunk)]
                at += len(chunk)
                n = sum(t.shape[0] for t in chunk)
                raw = None
                for start, w, row in blocks:
                    lhs = jnp.concatenate([t[:, pl.ds(start, depth)] for t in mine], axis=0)
                    part = jnp.dot(
                        lhs, w[row : row + depth, pl.ds(first_column, tile)], preferred_element_type=jnp.float32
                    )
                    raw = part if raw is None else raw + part
                c, s = cos_ref[base : base + n], sin_ref[base : base + n]
                first, second = raw[:, :HEAD], raw[:, HEAD:]
                second = turned(second, c, s) if queries else second.astype(jnp.bfloat16)
                out_ref[base : base + n, pl.ds(out_column, HEAD)] = turned(first, c, s)
                out_ref[base : base + n, pl.ds(out_column + HEAD, HEAD)] = second
                base += n

        if queries:

            def step(n, carry):
                at = pl.multiple_of(n * tile, tile)
                columns(at, at)
                return carry

            lax.fori_loop(0, 2, step, 0)
        else:
            columns(2 * tile, 0)

    vmem = pl.BlockSpec(memory_space=pltpu.VMEM)
    return pl.pallas_call(
        kernel,
        in_specs=[pl.BlockSpec(memory_space=pltpu.SMEM)] + [vmem] * (len(tokens) + len(flat) + 2),
        out_specs=vmem,
        out_shape=jax.ShapeDtypeStruct((rows, out_width), jnp.bfloat16),
        compiler_params=pltpu.CompilerParams(vmem_limit_bytes=PROJECT_VMEM),
        cost_estimate=pl.CostEstimate(
            flops=2 * rows * width * out_width, transcendentals=0, bytes_accessed=2 * (rows * width + width * out_width)
        ),
    )(place, *tokens, *flat, cos_table, sin_table)


def best_of(s):
    best = s[:, :HEAD]
    for lane in range(HEAD, s.shape[1], HEAD):
        best = jnp.maximum(best, s[:, lane : lane + HEAD])
    return best


def key_scores(s_ref, stacked, kv):
    at = 0
    for p in kv:
        n = p.shape[0]
        s_ref[:, at : at + n] = lax.dot_general(
            stacked, p[:, :HEAD], (((1,), (1,)), ((), ())), preferred_element_type=jnp.float32
        )
        at += n


def values_and_ones(kv):
    v = jnp.concatenate([p[:, HEAD:] for p in kv], axis=0)
    return jnp.concatenate([v, jnp.ones_like(v)], axis=1)


def weigh(scores, v):
    probs = [jnp.exp2((s - less) * LOG2E_SCALE).astype(jnp.bfloat16) for s, less in scores]
    return jnp.dot(jnp.concatenate(probs, axis=1), v, preferred_element_type=jnp.float32)


def attend_own(place, q_early, q_late, kv_early, kv_late, layout):
    heads = GROUP
    total = kv_early.shape[0] + kv_late.shape[0]
    rows = total // GROUP
    early = kv_early.shape[0]

    def kernel(place_ref, qe_ref, ql_ref, ke_ref, kl_ref, sums_ref, tops_ref, q_ref, s_ref):
        g, order = place_ref[1], pl.program_id(0)

        def sort():
            at = 0
            for j, first, n in layout:
                src = qe_ref[at : at + n] if at < early else ql_ref[at - early : at - early + n]
                q_ref[j * rows + first : j * rows + first + n] = src
                at += n

        pl.when(order == 0)(sort)
        at = pl.multiple_of(order * rows, rows)
        stacked = jnp.concatenate([q_ref[pl.ds(at, rows), h * HEAD : (h + 1) * HEAD] for h in range(heads)], axis=0)
        key_scores(s_ref, stacked, (ke_ref, kl_ref))
        v = values_and_ones((ke_ref, kl_ref))
        for h in range(heads):
            mine = slice(h * rows, (h + 1) * rows)
            scores, top, at = [], None, 0
            for j, first, n in layout:
                s = s_ref[mine, at : at + n]
                at += n
                ahead = lax.broadcasted_iota(jnp.int32, s.shape, 0) - lax.broadcasted_iota(jnp.int32, s.shape, 1)
                s = jnp.where(ahead >= ((g ^ j) - (g ^ order)) * rows + first, s, NEG)
                scores.append(s)
                top = best_of(s) if top is None else jnp.maximum(top, best_of(s))
            top = jnp.max(top, axis=1, keepdims=True)
            sums_ref[order, :, 2 * h * HEAD : 2 * (h + 1) * HEAD] = weigh([(s, top) for s in scores], v)
            tops_ref[order, :, h * HEAD : (h + 1) * HEAD] = jnp.broadcast_to(top, (rows, HEAD))

    vmem = pl.BlockSpec(memory_space=pltpu.VMEM)
    return pl.pallas_call(
        kernel,
        grid=(GROUP,),
        in_specs=[pl.BlockSpec(memory_space=pltpu.SMEM)] + [vmem] * 4,
        out_specs=[vmem] * 3,
        out_shape=[
            jax.ShapeDtypeStruct((GROUP, rows, 2 * heads * HEAD), jnp.float32),
            jax.ShapeDtypeStruct((GROUP, rows, heads * HEAD), jnp.float32),
            jax.ShapeDtypeStruct((total, heads * HEAD), jnp.bfloat16),
        ],
        scratch_shapes=[pltpu.VMEM((heads * rows, total), jnp.float32)],
        compiler_params=pltpu.CompilerParams(vmem_limit_bytes=16 << 20),
        cost_estimate=pl.CostEstimate(
            flops=8 * total * heads * HEAD * total, transcendentals=total * heads * total, bytes_accessed=3 << 20
        ),
    )(place, q_early, q_late, kv_early, kv_late)


def attend_below(place, sums, tops, queries, below, piece):
    heads = GROUP
    rows = queries.shape[0] // GROUP
    flat = [p for slab in below for p in slab]
    total = sum(p.shape[0] for p in flat)

    def kernel(place_ref, sums_ref, tops_ref, q_ref, *refs):
        kv = refs[: len(flat)]
        out_ref, s_ref = refs[len(flat) :]
        z = place_ref[0]
        first_row = piece * rows
        stacked = jnp.concatenate(
            [q_ref[first_row : first_row + rows, h * HEAD : (h + 1) * HEAD] for h in range(heads)], axis=0
        )
        key_scores(s_ref, stacked, kv)
        v = values_and_ones(kv)
        for h in range(heads):
            mine = slice(h * rows, (h + 1) * rows)
            old = tops_ref[piece, :, h * HEAD : h * HEAD + 1]
            found, top, at = [], tops_ref[piece, :, h * HEAD : (h + 1) * HEAD], 0
            for d, slab in enumerate(below, start=1):
                n = sum(p.shape[0] for p in slab)
                s = s_ref[mine, at : at + n]
                at += n
                found.append((s, z >= d))
                top = jnp.maximum(top, jnp.where(z >= d, best_of(s), NEG))
            top = jnp.max(top, axis=1, keepdims=True)
            mixed = weigh([(s, jnp.where(visible, top, -NEG)) for s, visible in found], v)
            mixed = mixed + sums_ref[piece, :, 2 * h * HEAD : 2 * (h + 1) * HEAD] * jnp.exp2((old - top) * LOG2E_SCALE)
            out_ref[:, h * HEAD : (h + 1) * HEAD] = (mixed[:, :HEAD] / mixed[:, HEAD:]).astype(jnp.bfloat16)

    vmem = pl.BlockSpec(memory_space=pltpu.VMEM)
    return pl.pallas_call(
        kernel,
        in_specs=[pl.BlockSpec(memory_space=pltpu.SMEM)] + [vmem] * (3 + len(flat)),
        out_specs=vmem,
        out_shape=jax.ShapeDtypeStruct((rows, heads * HEAD), jnp.bfloat16),
        scratch_shapes=[pltpu.VMEM((heads * rows, total), jnp.float32)],
        compiler_params=pltpu.CompilerParams(vmem_limit_bytes=28 << 20),
        cost_estimate=pl.CostEstimate(
            flops=8 * rows * heads * HEAD * total, transcendentals=rows * heads * total, bytes_accessed=3 << 20
        ),
    )(place, sums, tops, queries, *flat)


def section_tick(tokens, norm_gain, w_query, w_key, w_value):
    rank = lax.axis_index("seq")
    z, g = rank // GROUP, rank % GROUP
    place = jnp.stack([z, g]).astype(jnp.int32)
    rows = tokens.shape[1]
    half = rows // 2

    def columns(j):
        c = g ^ j
        take = lambda w, n: lax.dynamic_slice_in_dim(w[0], c * n, n, 1)
        return jnp.concatenate([take(w_query, 4 * HEAD), take(w_key, HEAD), take(w_value, HEAD)], axis=1)

    got = []
    for j in (1, 2, 3):
        got.append(near(columns(j), j))
    chip = jnp.concatenate([columns(0), got[0]], axis=0)
    other = jnp.concatenate([got[1], got[2]], axis=0)
    chip_left = along(chip, 1)
    chip_right = along(chip, -1)
    other_left = along(other, 1)
    other_right = along(other, -1)
    chip_far = along(chip_left, 1)
    other_far = along(other_right, -1)
    weights = [[chip, other], [chip_right, other_right], [chip_far, other_far], [chip_left, other_left]]

    normed = normalize(tokens[0], norm_gain[0])
    side = near(normed, 1)
    across, corner = [], []
    for i in range(2):
        across.append(near(normed[i * half : (i + 1) * half], 2))
    for i in range(2):
        corner.append(near(across[i], 1))

    early = [(0, 0, rows), (1, 0, rows), (2, 0, half), (3, 0, half)]
    late = [(2, half, half), (3, half, half)]
    tables_early = rope_tables(z, g, rows, early)
    tables_late = rope_tables(z, g, rows, late)
    chunks_early = [[normed, side, across[0], corner[0]]]
    chunks_late = [[across[1], corner[1]]]
    kv_early = project(place, chunks_early, weights, *tables_early, False)
    q_early = project(place, chunks_early, weights, *tables_early, True)
    kv_late = project(place, chunks_late, weights, *tables_late, False)
    q_late = project(place, chunks_late, weights, *tables_late, True)

    cut = kv_early.shape[0] // 2
    one = upward(kv_early, [(0, 1), (1, 2), (2, 3)])
    three = upward(kv_early, [(0, 3), (1, 0)])
    two_a = upward(one[:cut], [(1, 2), (2, 3)])
    two_b = upward(three[cut:], [(3, 2), (0, 3)])
    late_one = upward(kv_late, [(0, 1), (1, 2), (2, 3)])
    late_two = upward(kv_late, [(0, 2), (1, 3)])
    late_three = upward(kv_late, [(0, 3)])
    below = [[one, late_one], [two_a, two_b, late_two], [three, late_three]]

    sums, tops, queries = attend_own(place, q_early, q_late, kv_early, kv_late, early + late)
    out = jnp.zeros((rows, GROUP * GROUP * HEAD), jnp.bfloat16)
    for k in range(GROUP):
        mixed = attend_below(place, sums, tops, queries, below, k)
        arrived = onward(mixed, k)
        out = lax.dynamic_update_slice(out, arrived, (0, (g ^ k) * GROUP * HEAD))
    return out[None]


def solution(mesh):
    return jax.shard_map(
        section_tick,
        mesh=mesh,
        in_specs=(
            P("section", "seq", None),
            P("section", None),
            P("section", "seq", None),
            P("section", "seq", None),
            P("section", "seq", None),
        ),
        out_specs=P("section", "seq", None),
        check_vma=False,
    )
```

profile of v0, /device:TPU:0, one launch (start us, length us, event | category | flops | bytes accessed | tf_op | source)
XLA Modules:
  0.0 209.7 jit_solution(10309139702030373068)
XLA Ops:
  0.0 2.2 %fusion = f32[256]{0:T(256)S(1)} fusion(bf16[1,256,4096]{2,1,0:T(8,128)(2,1)} %param.5), kind=kLoop, calls=%fused_computation.2 | loop fusion | flops 3145472 | bytes 2098176 | tf_op jit(solution)/shard_map/reduce_sum | solution.py:41
  10.7 51.6 %collective-permute-done.4 = bf16[256,768]{1,0:T(8,128)(2,1)S(1)} collective-permute-done((bf16[256,768]{1,0:T(8,128)(2,1)S(1)}, bf16[256,768]{1,0:T(8,128)(2,1)S(1)}, u32[]{:S(2)}, u32[]{:S(2)}) %collective-permute-start.4) | collective-permute-done | bytes 393248 | tf_op jit(solution)/shard_map/ppermute | solution.py:20
  63.1 5.7 %collective-permute-done.5 = bf16[256,768]{1,0:T(8,128)(2,1)S(1)} collective-permute-done((bf16[256,768]{1,0:T(8,128)(2,1)S(1)}, bf16[256,768]{1,0:T(8,128)(2,1)S(1)}, u32[]{:S(2)}, u32[]{:S(2)}) %collective-permute-start.5) | collective-permute-done | bytes 393248 | tf_op jit(solution)/shard_map/ppermute | solution.py:20
  71.5 2.1 %collective-permute-start.7 = (bf16[512,768]{1,0:T(8,128)(2,1)}, bf16[512,768]{1,0:T(8,128)(2,1)}, u32[]{:S(2)}, u32[]{:S(2)}) collective-permute-start(bf16[512,768]{1,0:T(8,128)(2,1)} %constant_dynamic-update-slice_fusion.refs_5_.refs_3_), channel_id=1, source_target_pairs={{0,12},{1,13},{2,14},{3,15},{4,0},{5,1},{6,2},{7,3},{8,4},{9,5},{1... | collective-permute-start | bytes 2359304 | tf_op jit(solution)/shard_map/ppermute | solution.py:25
  73.8 3.2 %collective-permute-start.6 = (bf16[512,768]{1,0:T(8,128)(2,1)S(1)}, bf16[512,768]{1,0:T(8,128)(2,1)}, u32[]{:S(2)}, u32[]{:S(2)}) collective-permute-start(bf16[512,768]{1,0:T(8,128)(2,1)S(1)} %pad_maximum_fusion.refs_4_.refs_2_), channel_id=1, source_target_pairs={{0,12},{1,13},{2,14},{3,15},{4,0},{5,1},{6,2},{7,3},{8,4},{9,5},{1... | collective-permute-start | bytes 2359304 | tf_op jit(solution)/shard_map/ppermute | solution.py:25
  77.1 15.2 %collective-permute-done.11.refs_11_.refs_9_ = bf16[512,768]{1,0:T(8,128)(2,1)} collective-permute-done((bf16[512,768]{1,0:T(8,128)(2,1)}, bf16[512,768]{1,0:T(8,128)(2,1)}, u32[]{:S(2)}, u32[]{:S(2)}) %collective-permute-start.11) | collective-permute-done | bytes 786464 | tf_op jit(solution)/shard_map/ppermute | solution.py:25
  92.8 16.3 %collective-permute-done.8.refs_10_.refs_8_ = bf16[512,768]{1,0:T(8,128)(2,1)} collective-permute-done((bf16[512,768]{1,0:T(8,128)(2,1)S(1)}, bf16[512,768]{1,0:T(8,128)(2,1)}, u32[]{:S(2)}, u32[]{:S(2)}) %collective-permute-start.8) | collective-permute-done | bytes 786464 | tf_op jit(solution)/shard_map/ppermute | solution.py:25
  113.3 15.7 %collective-permute-done.10.refs_9_.refs_7_ = bf16[512,768]{1,0:T(8,128)(2,1)S(1)} collective-permute-done((bf16[512,768]{1,0:T(8,128)(2,1)}, bf16[512,768]{1,0:T(8,128)(2,1)S(1)}, u32[]{:S(2)}, u32[]{:S(2)}) %collective-permute-start.10) | collective-permute-done | bytes 786464 | tf_op jit(solution)/shard_map/ppermute | solution.py:25
  128.9 2.5 %collective-permute-done.9.refs_8_.refs_6_ = bf16[512,768]{1,0:T(8,128)(2,1)S(1)} collective-permute-done((bf16[512,768]{1,0:T(8,128)(2,1)}, bf16[512,768]{1,0:T(8,128)(2,1)S(1)}, u32[]{:S(2)}, u32[]{:S(2)}) %collective-permute-start.9) | collective-permute-done | bytes 786464 | tf_op jit(solution)/shard_map/ppermute | solution.py:25
  131.4 3.5 %shard_map.58.kl_ref = bf16[256,256]{1,0:T(8,128)(2,1)S(1)} custom-call(s32[2]{0:T(128)S(1)} %pad_add_fusion.place_ref, bf16[128,4096]{1,0:T(8,128)(2,1)} %collective-permute-done.12.refs_0_, bf16[128,4096]{1,0:T(8,128)(2,1)} %collective-permute-done.13.refs_1_, bf16[512,768]{1,0:T(8,128)(2,1)S(1)} %pad_maximum_fusion.refs_4_.refs_2_, ...), custom_call_target="tpu_custom_call" | custom-call | flops 536870912 | bytes 4194304 | tf_op jit(solution)/shard_map/pallas_call | solution.py:120
  135.0 2.2 %collective-permute-start.20 = (bf16[256,256]{1,0:T(8,128)(2,1)S(1)}, bf16[256,256]{1,0:T(8,128)(2,1)S(1)}, u32[]{:S(2)}, u32[]{:S(2)}) collective-permute-start(bf16[256,256]{1,0:T(8,128)(2,1)S(1)} %shard_map.58.kl_ref), channel_id=1, source_target_pairs={{0,12},{1,13},{2,14},{3,15},{16,28},{17,29},{18,30},{19,31},{32,44... | collective-permute-start | bytes 393224 | tf_op jit(solution)/shard_map/ppermute | solution.py:29
  138.5 2.8 %collective-permute-start.15 = (bf16[256,256]{1,0:T(8,128)(2,1)S(1)}, bf16[256,256]{1,0:T(8,128)(2,1)S(1)}, u32[]{:S(2)}, u32[]{:S(2)}) collective-permute-start(bf16[256,256]{1,0:T(8,128)(2,1)S(1)} %shard_map.58.kl_ref), channel_id=1, source_target_pairs={{0,4},{1,5},{2,6},{3,7},{4,8},{5,9},{6,10},{7,11},{8,12},{9,13},{1... | collective-permute-start | bytes 393224 | tf_op jit(solution)/shard_map/ppermute | solution.py:29
  141.3 4.9 %shard_map.57.ke_ref = bf16[768,256]{1,0:T(8,128)(2,1)S(1)} custom-call(s32[2]{0:T(128)S(1)} %pad_add_fusion.place_ref, bf16[256,4096]{1,0:T(8,128)(2,1)S(1)} %fusion.2.refs_0_, bf16[256,4096]{1,0:T(8,128)(2,1)} %collective-permute-done.refs_1_, bf16[128,4096]{1,0:T(8,128)(2,1)} %collective-permute-done.1.refs_2_, ...), custom_call_target="tpu_custom_call" | custom-call | flops 1610612736 | bytes 8388608 | tf_op jit(solution)/shard_map/pallas_call | solution.py:120
  148.1 4.1 %collective-permute-start.14 = (bf16[768,256]{1,0:T(8,128)(2,1)S(1)}, bf16[768,256]{1,0:T(8,128)(2,1)S(1)}, u32[]{:S(2)}, u32[]{:S(2)}) collective-permute-start(bf16[768,256]{1,0:T(8,128)(2,1)S(1)} %shard_map.57.ke_ref), channel_id=1, source_target_pairs={{0,4},{1,5},{2,6},{3,7},{4,8},{5,9},{6,10},{7,11},{8,12},{9,13},{1... | collective-permute-start | bytes 1179656 | tf_op jit(solution)/shard_map/ppermute | solution.py:29
  152.2 4.4 %shard_map.56.ql_ref = bf16[256,512]{1,0:T(8,128)(2,1)S(1)} custom-call(s32[2]{0:T(128)S(1)} %pad_add_fusion.place_ref, bf16[128,4096]{1,0:T(8,128)(2,1)} %collective-permute-done.12.refs_0_, bf16[128,4096]{1,0:T(8,128)(2,1)} %collective-permute-done.13.refs_1_, bf16[512,768]{1,0:T(8,128)(2,1)S(1)} %pad_maximum_fusion.refs_4_.refs_2_, ...), custom_call_target="tpu_custom_call" | custom-call | flops 1073741824 | bytes 6291456 | tf_op jit(solution)/shard_map/pallas_call | solution.py:120
  156.6 6.9 %shard_map.55.qe_ref = bf16[768,512]{1,0:T(8,128)(2,1)S(1)} custom-call(s32[2]{0:T(128)S(1)} %pad_add_fusion.place_ref, bf16[256,4096]{1,0:T(8,128)(2,1)S(1)} %fusion.2.refs_0_, bf16[256,4096]{1,0:T(8,128)(2,1)} %collective-permute-done.refs_1_, bf16[128,4096]{1,0:T(8,128)(2,1)} %collective-permute-done.1.refs_2_, ...), custom_call_target="tpu_custom_call" | custom-call | flops 3221225472 | bytes 10485760 | tf_op jit(solution)/shard_map/pallas_call | solution.py:120
  165.6 7.4 %shard_map.59 = (f32[4,256,1024]{2,1,0:T(8,128)S(1)}, f32[4,256,512]{2,1,0:T(8,128)S(1)}, bf16[1024,512]{1,0:T(8,128)(2,1)S(1)}) custom-call(s32[2]{0:T(128)S(1)} %pad_add_fusion.place_ref, bf16[768,512]{1,0:T(8,128)(2,1)S(1)} %shard_map.55.qe_ref, bf16[256,512]{1,0:T(8,128)(2,1)S(1)} %shard_map.56.ql_ref, bf16[768,256]{1,0:T(8,128)(2,1)S(1)} %shard_map.57.ke_ref, ...), custom_call_target="tpu_custom_call" | custom-call | flops 4294967296 | bytes 3145728 | tf_op jit(solution)/shard_map/pallas_call | solution.py:195
  173.0 5.1 %shard_map.60 = bf16[256,512]{1,0:T(8,128)(2,1)S(1)} custom-call(s32[2]{0:T(128)S(1)} %pad_add_fusion.place_ref, f32[4,256,1024]{2,1,0:T(8,128)S(1)} %get-tuple-element.8.sums_ref, f32[4,256,512]{2,1,0:T(8,128)S(1)} %get-tuple-element.9.tops_ref, bf16[1024,512]{1,0:T(8,128)(2,1)S(1)} %get-tuple-element.10.q_ref, ...), custom_call_target="tpu_custom_call" | custom-call | flops 3221225472 | bytes 3145728 | tf_op jit(solution)/shard_map/pallas_call | solution.py:245
  179.9 5.1 %shard_map.61 = bf16[256,512]{1,0:T(8,128)(2,1)S(1)} custom-call(s32[2]{0:T(128)S(1)} %pad_add_fusion.place_ref, f32[4,256,1024]{2,1,0:T(8,128)S(1)} %get-tuple-element.8.sums_ref, f32[4,256,512]{2,1,0:T(8,128)S(1)} %get-tuple-element.9.tops_ref, bf16[1024,512]{1,0:T(8,128)(2,1)S(1)} %get-tuple-element.10.q_ref, ...), custom_call_target="tpu_custom_call" | custom-call | flops 3221225472 | bytes 3145728 | tf_op jit(solution)/shard_map/pallas_call | solution.py:245
  185.0 5.1 %shard_map.62 = bf16[256,512]{1,0:T(8,128)(2,1)S(1)} custom-call(s32[2]{0:T(128)S(1)} %pad_add_fusion.place_ref, f32[4,256,1024]{2,1,0:T(8,128)S(1)} %get-tuple-element.8.sums_ref, f32[4,256,512]{2,1,0:T(8,128)S(1)} %get-tuple-element.9.tops_ref, bf16[1024,512]{1,0:T(8,128)(2,1)S(1)} %get-tuple-element.10.q_ref, ...), custom_call_target="tpu_custom_call" | custom-call | flops 3221225472 | bytes 3145728 | tf_op jit(solution)/shard_map/pallas_call | solution.py:245
  190.1 3.1 %collective-permute-start.23 = (bf16[256,512]{1,0:T(8,128)(2,1)S(1)}, bf16[256,512]{1,0:T(8,128)(2,1)S(1)}, u32[]{:S(2)}, u32[]{:S(2)}) collective-permute-start(bf16[256,512]{1,0:T(8,128)(2,1)S(1)} %shard_map.62), channel_id=1, source_target_pairs={{0,18},{1,19},{2,16},{3,17},{4,22},{5,23},{6,20},{7,21},{8,26},{9,... | collective-permute-start | bytes 786440 | tf_op jit(solution)/shard_map/ppermute | solution.py:36
  193.1 5.1 %shard_map.63 = bf16[256,512]{1,0:T(8,128)(2,1)S(1)} custom-call(s32[2]{0:T(128)S(1)} %pad_add_fusion.place_ref, f32[4,256,1024]{2,1,0:T(8,128)S(1)} %get-tuple-element.8.sums_ref, f32[4,256,512]{2,1,0:T(8,128)S(1)} %get-tuple-element.9.tops_ref, bf16[1024,512]{1,0:T(8,128)(2,1)S(1)} %get-tuple-element.10.q_ref, ...), custom_call_target="tpu_custom_call" | custom-call | flops 3221225472 | bytes 3145728 | tf_op jit(solution)/shard_map/pallas_call | solution.py:245
  198.2 3.7 %collective-permute-start.24 = (bf16[256,512]{1,0:T(8,128)(2,1)S(1)}, bf16[256,512]{1,0:T(8,128)(2,1)S(1)}, u32[]{:S(2)}, u32[]{:S(2)}) collective-permute-start(bf16[256,512]{1,0:T(8,128)(2,1)S(1)} %shard_map.63), channel_id=1, source_target_pairs={{0,19},{1,18},{2,17},{3,16},{4,23},{5,22},{6,21},{7,20},{8,27},{9,... | collective-permute-start | bytes 786440 | tf_op jit(solution)/shard_map/ppermute | solution.py:36
  202.3 6.7 %collective-permute-done.24 = bf16[256,512]{1,0:T(8,128)(2,1)S(1)} collective-permute-done((bf16[256,512]{1,0:T(8,128)(2,1)S(1)}, bf16[256,512]{1,0:T(8,128)(2,1)S(1)}, u32[]{:S(2)}, u32[]{:S(2)}) %collective-permute-start.24) | collective-permute-done | bytes 262176 | tf_op jit(solution)/shard_map/ppermute | solution.py:36
  (75 shorter events, 25.0 us)
Async XLA Ops:
  5.2 68.5 %collective-permute-start.12 = (bf16[128,4096]{1,0:T(8,128)(2,1)}, bf16[128,4096]{1,0:T(8,128)(2,1)}, u32[]{:S(2)}, u32[]{:S(2)}) collective-permute-start(bf16[128,4096]{1,0:T(8,128)(2,1)} %get-tuple-element.11), channel_id=1, source_target_pairs={{0,2},{1,3},{2,0},{3,1},{4,6},{5,7},{6,4},{7,5},{8,10},{9,11},{10,... | collective-permute-start | bytes 3145736 | tf_op jit(solution)/shard_map/ppermute | solution.py:20
  6.9 66.9 %collective-permute-start.1 = (bf16[128,4096]{1,0:T(8,128)(2,1)}, bf16[128,4096]{1,0:T(8,128)(2,1)}, u32[]{:S(2)}, u32[]{:S(2)}) collective-permute-start(bf16[128,4096]{1,0:T(8,128)(2,1)} %get-tuple-element.12), channel_id=1, source_target_pairs={{0,2},{1,3},{2,0},{3,1},{4,6},{5,7},{6,4},{7,5},{8,10},{9,11},{10,... | collective-permute-start | bytes 3145736 | tf_op jit(solution)/shard_map/ppermute | solution.py:20
  8.3 54.0 %collective-permute-start.4 = (bf16[256,768]{1,0:T(8,128)(2,1)S(1)}, bf16[256,768]{1,0:T(8,128)(2,1)S(1)}, u32[]{:S(2)}, u32[]{:S(2)}) collective-permute-start(bf16[256,768]{1,0:T(8,128)(2,1)S(1)} %pad_maximum_fusion.2), channel_id=1, source_target_pairs={{0,2},{1,3},{2,0},{3,1},{4,6},{5,7},{6,4},{7,5},{8,10},{9,11},{10,... | collective-permute-start | bytes 1179656 | tf_op jit(solution)/shard_map/ppermute | solution.py:20
  10.1 58.7 %collective-permute-start.5 = (bf16[256,768]{1,0:T(8,128)(2,1)S(1)}, bf16[256,768]{1,0:T(8,128)(2,1)S(1)}, u32[]{:S(2)}, u32[]{:S(2)}) collective-permute-start(bf16[256,768]{1,0:T(8,128)(2,1)S(1)} %pad_maximum_fusion.3), channel_id=1, source_target_pairs={{0,3},{1,2},{2,1},{3,0},{4,7},{5,6},{6,5},{7,4},{8,11},{9,10},{10,... | collective-permute-start | bytes 1179656 | tf_op jit(solution)/shard_map/ppermute | solution.py:20
  10.2 61.3 %collective-permute-start.3 = (bf16[256,768]{1,0:T(8,128)(2,1)S(1)}, bf16[256,768]{1,0:T(8,128)(2,1)S(1)}, u32[]{:S(2)}, u32[]{:S(2)}) collective-permute-start(bf16[256,768]{1,0:T(8,128)(2,1)S(1)} %pad_maximum_fusion.1), channel_id=1, source_target_pairs={{0,1},{1,0},{2,3},{3,2},{4,5},{5,4},{6,7},{7,6},{8,9},{9,8},{10,11... | collective-permute-start | bytes 1179656 | tf_op jit(solution)/shard_map/ppermute | solution.py:20
  62.3 78.9 %collective-permute-start = (bf16[256,4096]{1,0:T(8,128)(2,1)S(1)}, bf16[256,4096]{1,0:T(8,128)(2,1)}, u32[]{:S(2)}, u32[]{:S(2)}) collective-permute-start(bf16[256,4096]{1,0:T(8,128)(2,1)S(1)} %fusion.2.refs_0_), channel_id=1, source_target_pairs={{0,1},{1,0},{2,3},{3,2},{4,5},{5,4},{6,7},{7,6},{8,9},{9,8},{10,11... | collective-permute-start | bytes 6291464 | tf_op jit(solution)/shard_map/ppermute | solution.py:20
  69.6 22.7 %collective-permute-start.11 = (bf16[512,768]{1,0:T(8,128)(2,1)}, bf16[512,768]{1,0:T(8,128)(2,1)}, u32[]{:S(2)}, u32[]{:S(2)}) collective-permute-start(bf16[512,768]{1,0:T(8,128)(2,1)} %constant_dynamic-update-slice_fusion.refs_5_.refs_3_), channel_id=1, source_target_pairs={{0,4},{1,5},{2,6},{3,7},{4,8},{5,9},{6,10},{7,11},{8,12},{9,13},{1... | collective-permute-start | bytes 2359304 | tf_op jit(solution)/shard_map/ppermute | solution.py:25
  71.5 21.0 %collective-permute-start.7 = (bf16[512,768]{1,0:T(8,128)(2,1)}, bf16[512,768]{1,0:T(8,128)(2,1)}, u32[]{:S(2)}, u32[]{:S(2)}) collective-permute-start(bf16[512,768]{1,0:T(8,128)(2,1)} %constant_dynamic-update-slice_fusion.refs_5_.refs_3_), channel_id=1, source_target_pairs={{0,12},{1,13},{2,14},{3,15},{4,0},{5,1},{6,2},{7,3},{8,4},{9,5},{1... | collective-permute-start | bytes 2359304 | tf_op jit(solution)/shard_map/ppermute | solution.py:25
  73.7 35.4 %collective-permute-start.8 = (bf16[512,768]{1,0:T(8,128)(2,1)S(1)}, bf16[512,768]{1,0:T(8,128)(2,1)}, u32[]{:S(2)}, u32[]{:S(2)}) collective-permute-start(bf16[512,768]{1,0:T(8,128)(2,1)S(1)} %pad_maximum_fusion.refs_4_.refs_2_), channel_id=1, source_target_pairs={{0,4},{1,5},{2,6},{3,7},{4,8},{5,9},{6,10},{7,11},{8,12},{9,13},{1... | collective-permute-start | bytes 2359304 | tf_op jit(solution)/shard_map/ppermute | solution.py:25
  73.8 37.2 %collective-permute-start.6 = (bf16[512,768]{1,0:T(8,128)(2,1)S(1)}, bf16[512,768]{1,0:T(8,128)(2,1)}, u32[]{:S(2)}, u32[]{:S(2)}) collective-permute-start(bf16[512,768]{1,0:T(8,128)(2,1)S(1)} %pad_maximum_fusion.refs_4_.refs_2_), channel_id=1, source_target_pairs={{0,12},{1,13},{2,14},{3,15},{4,0},{5,1},{6,2},{7,3},{8,4},{9,5},{1... | collective-permute-start | bytes 2359304 | tf_op jit(solution)/shard_map/ppermute | solution.py:25
  92.3 39.1 %collective-permute-start.13 = (bf16[128,4096]{1,0:T(8,128)(2,1)}, bf16[128,4096]{1,0:T(8,128)(2,1)}, u32[]{:S(2)}, u32[]{:S(2)}) collective-permute-start(bf16[128,4096]{1,0:T(8,128)(2,1)} %collective-permute-done.12.refs_0_), channel_id=1, source_target_pairs={{0,1},{1,0},{2,3},{3,2},{4,5},{5,4},{6,7},{7,6},{8,9},{9,8},{10,11... | collective-permute-start | bytes 3145736 | tf_op jit(solution)/shard_map/ppermute | solution.py:20
  92.5 48.7 %collective-permute-start.2 = (bf16[128,4096]{1,0:T(8,128)(2,1)}, bf16[128,4096]{1,0:T(8,128)(2,1)S(1)}, u32[]{:S(2)}, u32[]{:S(2)}) collective-permute-start(bf16[128,4096]{1,0:T(8,128)(2,1)} %collective-permute-done.1.refs_2_), channel_id=1, source_target_pairs={{0,1},{1,0},{2,3},{3,2},{4,5},{5,4},{6,7},{7,6},{8,9},{9,8},{10,11... | collective-permute-start | bytes 3145736 | tf_op jit(solution)/shard_map/ppermute | solution.py:20
  109.1 19.8 %collective-permute-start.10 = (bf16[512,768]{1,0:T(8,128)(2,1)}, bf16[512,768]{1,0:T(8,128)(2,1)S(1)}, u32[]{:S(2)}, u32[]{:S(2)}) collective-permute-start(bf16[512,768]{1,0:T(8,128)(2,1)} %collective-permute-done.7.refs_7_.refs_5_), channel_id=1, source_target_pairs={{0,12},{1,13},{2,14},{3,15},{4,0},{5,1},{6,2},{7,3},{8,4},{9,5},{1... | collective-permute-start | bytes 2359304 | tf_op jit(solution)/shard_map/ppermute | solution.py:25
  111.0 20.5 %collective-permute-start.9 = (bf16[512,768]{1,0:T(8,128)(2,1)}, bf16[512,768]{1,0:T(8,128)(2,1)S(1)}, u32[]{:S(2)}, u32[]{:S(2)}) collective-permute-start(bf16[512,768]{1,0:T(8,128)(2,1)} %collective-permute-done.8.refs_10_.refs_8_), channel_id=1, source_target_pairs={{0,4},{1,5},{2,6},{3,7},{4,8},{5,9},{6,10},{7,11},{8,12},{9,13},{1... | collective-permute-start | bytes 2359304 | tf_op jit(solution)/shard_map/ppermute | solution.py:25
  135.0 38.0 %collective-permute-start.20 = (bf16[256,256]{1,0:T(8,128)(2,1)S(1)}, bf16[256,256]{1,0:T(8,128)(2,1)S(1)}, u32[]{:S(2)}, u32[]{:S(2)}) collective-permute-start(bf16[256,256]{1,0:T(8,128)(2,1)S(1)} %shard_map.58.kl_ref), channel_id=1, source_target_pairs={{0,12},{1,13},{2,14},{3,15},{16,28},{17,29},{18,30},{19,31},{32,44... | collective-permute-start | bytes 393224 | tf_op jit(solution)/shard_map/ppermute | solution.py:29
  137.2 35.8 %collective-permute-start.19 = (bf16[256,256]{1,0:T(8,128)(2,1)S(1)}, bf16[256,256]{1,0:T(8,128)(2,1)S(1)}, u32[]{:S(2)}, u32[]{:S(2)}) collective-permute-start(bf16[256,256]{1,0:T(8,128)(2,1)S(1)} %shard_map.58.kl_ref), channel_id=1, source_target_pairs={{0,8},{1,9},{2,10},{3,11},{4,12},{5,13},{6,14},{7,15},{16,24},{17,... | collective-permute-start | bytes 393224 | tf_op jit(solution)/shard_map/ppermute | solution.py:29
  138.5 34.5 %collective-permute-start.15 = (bf16[256,256]{1,0:T(8,128)(2,1)S(1)}, bf16[256,256]{1,0:T(8,128)(2,1)S(1)}, u32[]{:S(2)}, u32[]{:S(2)}) collective-permute-start(bf16[256,256]{1,0:T(8,128)(2,1)S(1)} %shard_map.58.kl_ref), channel_id=1, source_target_pairs={{0,4},{1,5},{2,6},{3,7},{4,8},{5,9},{6,10},{7,11},{8,12},{9,13},{1... | collective-permute-start | bytes 393224 | tf_op jit(solution)/shard_map/ppermute | solution.py:29
  146.2 17.4 %collective-permute-start.17 = (bf16[768,256]{1,0:T(8,128)(2,1)S(1)}, bf16[768,256]{1,0:T(8,128)(2,1)S(1)}, u32[]{:S(2)}, u32[]{:S(2)}) collective-permute-start(bf16[768,256]{1,0:T(8,128)(2,1)S(1)} %shard_map.57.ke_ref), channel_id=1, source_target_pairs={{0,12},{1,13},{2,14},{3,15},{4,0},{5,1},{6,2},{7,3},{16,28},{17,29... | collective-permute-start | bytes 1179656 | tf_op jit(solution)/shard_map/ppermute | solution.py:29
  148.1 16.8 %collective-permute-start.14 = (bf16[768,256]{1,0:T(8,128)(2,1)S(1)}, bf16[768,256]{1,0:T(8,128)(2,1)S(1)}, u32[]{:S(2)}, u32[]{:S(2)}) collective-permute-start(bf16[768,256]{1,0:T(8,128)(2,1)S(1)} %shard_map.57.ke_ref), channel_id=1, source_target_pairs={{0,4},{1,5},{2,6},{3,7},{4,8},{5,9},{6,10},{7,11},{8,12},{9,13},{1... | collective-permute-start | bytes 1179656 | tf_op jit(solution)/shard_map/ppermute | solution.py:29
  163.6 9.4 %collective-permute-start.18 = (bf16[384,256]{1,0:T(8,128)(2,1)S(1)}, bf16[384,256]{1,0:T(8,128)(2,1)S(1)}, u32[]{:S(2)}, u32[]{:S(2)}) collective-permute-start(bf16[384,256]{1,0:T(8,128)(2,1)S(1)} %slice.19), channel_id=1, source_target_pairs={{12,8},{13,9},{14,10},{15,11},{0,12},{1,13},{2,14},{3,15},{28,24},... | collective-permute-start | bytes 589832 | tf_op jit(solution)/shard_map/ppermute | solution.py:29
  178.1 23.8 %collective-permute-start.21 = (bf16[256,512]{1,0:T(8,128)(2,1)S(1)}, bf16[256,512]{1,0:T(8,128)(2,1)S(1)}, u32[]{:S(2)}, u32[]{:S(2)}) collective-permute-start(bf16[256,512]{1,0:T(8,128)(2,1)S(1)} %shard_map.60), channel_id=1, source_target_pairs={{0,16},{1,17},{2,18},{3,19},{4,20},{5,21},{6,22},{7,23},{8,24},{9,... | collective-permute-start | bytes 786440 | tf_op jit(solution)/shard_map/ppermute | solution.py:36
  184.9 17.1 %collective-permute-start.22 = (bf16[256,512]{1,0:T(8,128)(2,1)S(1)}, bf16[256,512]{1,0:T(8,128)(2,1)S(1)}, u32[]{:S(2)}, u32[]{:S(2)}) collective-permute-start(bf16[256,512]{1,0:T(8,128)(2,1)S(1)} %shard_map.61), channel_id=1, source_target_pairs={{0,17},{1,16},{2,19},{3,18},{4,21},{5,20},{6,23},{7,22},{8,25},{9,... | collective-permute-start | bytes 786440 | tf_op jit(solution)/shard_map/ppermute | solution.py:36
  190.1 12.2 %collective-permute-start.23 = (bf16[256,512]{1,0:T(8,128)(2,1)S(1)}, bf16[256,512]{1,0:T(8,128)(2,1)S(1)}, u32[]{:S(2)}, u32[]{:S(2)}) collective-permute-start(bf16[256,512]{1,0:T(8,128)(2,1)S(1)} %shard_map.62), channel_id=1, source_target_pairs={{0,18},{1,19},{2,16},{3,17},{4,22},{5,23},{6,20},{7,21},{8,26},{9,... | collective-permute-start | bytes 786440 | tf_op jit(solution)/shard_map/ppermute | solution.py:36
  198.2 10.8 %collective-permute-start.24 = (bf16[256,512]{1,0:T(8,128)(2,1)S(1)}, bf16[256,512]{1,0:T(8,128)(2,1)S(1)}, u32[]{:S(2)}, u32[]{:S(2)}) collective-permute-start(bf16[256,512]{1,0:T(8,128)(2,1)S(1)} %shard_map.63), channel_id=1, source_target_pairs={{0,19},{1,18},{2,17},{3,16},{4,23},{5,22},{6,21},{7,20},{8,27},{9,... | collective-permute-start | bytes 786440 | tf_op jit(solution)/shard_map/ppermute | solution.py:36
  (6 other events, 24.4 us)
where the time goes:
time: 212 us; the launch traced here: 210 us
  waiting for transfers between devices  114 us (54%)
  Pallas kernels  47.3 us (22%)
  starting transfers between devices  37.2 us (18%)
  other arithmetic  5.95 us (3%)
  local copies, waits for them, and re-layouts  5.1 us (2%)
    ppermute x8, waiting for transfers between devices, near(): lax.ppermute(block, 'seq', [(r, r ^ bits) for r in range(RING * GROUP)])  57.3 us
    ppermute x6, waiting for transfers between devices, along(): lax.ppermute(block, 'seq', [(r, (r + step * GROUP) % n) for r in range(n)])  49.7 us
    pallas_call x4, Pallas kernels, attend_below(): pl.pallas_call(kernel, in_specs=[pl.BlockSpec(memory_space=pltpu.SMEM)] +...  20.2 us
    pallas_call x4, Pallas kernels, project(): pl.pallas_call(kernel, in_specs=[pl.BlockSpec(memory_space=pltpu.SMEM)] +...  19.7 us
    ppermute x7, starting transfers between devices, upward(): lax.ppermute(block, 'seq', [(a * GROUP + g, b * GROUP + g) for a, b in ro...  14.3 us
    ppermute x6, starting transfers between devices, along(): lax.ppermute(block, 'seq', [(r, (r + step * GROUP) % n) for r in range(n)])  9.36 us
    ppermute x4, starting transfers between devices, onward(): return lax.ppermute(block, ('section', 'seq'), route)  8.61 us
    pallas_call x1, Pallas kernels, attend_own(): pl.pallas_call(kernel, grid=(GROUP,), in_specs=[pl.BlockSpec(memory_space...  7.36 us
  transfers between devices with their start and end apart: 25, of which 8 were waited for; matrix products, arithmetic and copies ran while one was open for 2% of the time, Pallas kernels for 20%

commit v1 on v0

--- a/solution.py
+++ b/solution.py
@@ -13,7 +13,6 @@
 RING = 4
 LOG2E_SCALE = math.log2(math.e) / math.sqrt(HEAD)
 NEG = -1e30
-PROJECT_VMEM = 10 << 20
 
 
 def near(block, bits):
@@ -52,81 +51,122 @@
     return jnp.cos(angles), jnp.sin(angles) * sign[None, :]
 
 
-def weight_blocks(place_ref, weights, refs, depth):
-    z, g = place_ref[0], place_ref[1]
-    blocks, at = [], 0
-    for off, slab in enumerate(weights):
-        j = 0
-        for w in slab:
-            for row in range(0, w.shape[0], depth):
-                start = pl.multiple_of((((z + off) % RING) * GROUP + (g ^ j)) * depth, depth)
-                blocks.append((start, refs[at], row))
-                j += 1
-            at += 1
-    return blocks
-
-
 def turned(x, c, s):
     return (x * c + pltpu.roll(x, HEAD // 2, 1) * s).astype(jnp.bfloat16)
 
 
-def project(place, chunks, weights, cos_table, sin_table, queries):
-    tokens = [t for chunk in chunks for t in chunk]
-    rows = sum(t.shape[0] for t in tokens)
-    width = tokens[0].shape[1]
-    depth = width // (RING * GROUP)
-    flat = [w for slab in weights for w in slab]
-    tile = 2 * HEAD
-    out_width = 2 * tile if queries else tile
-
-    def kernel(place_ref, *refs):
-        tok = refs[: len(tokens)]
-        wts = refs[len(tokens) : len(tokens) + len(flat)]
-        cos_ref, sin_ref, out_ref = refs[len(tokens) + len(flat) :]
-        blocks = weight_blocks(place_ref, weights, wts, depth)
-
-        def columns(first_column, out_column):
-            at, base = 0, 0
-            for chunk in chunks:
-                mine = tok[at : at + len(chunk)]
-                at += len(chunk)
-                n = sum(t.shape[0] for t in chunk)
-                raw = None
-                for start, w, row in blocks:
-                    lhs = jnp.concatenate([t[:, pl.ds(start, depth)] for t in mine], axis=0)
-                    part = jnp.dot(
-                        lhs, w[row : row + depth, pl.ds(first_column, tile)], preferred_element_type=jnp.float32
-                    )
-                    raw = part if raw is None else raw + part
-                c, s = cos_ref[base : base + n], sin_ref[base : base + n]
-                first, second = raw[:, :HEAD], raw[:, HEAD:]
-                second = turned(second, c, s) if queries else second.astype(jnp.bfloat16)
-                out_ref[base : base + n, pl.ds(out_column, HEAD)] = turned(first, c, s)
-                out_ref[base : base + n, pl.ds(out_column + HEAD, HEAD)] = second
-                base += n
-
-        if queries:
-
-            def step(n, carry):
-                at = pl.multiple_of(n * tile, tile)
-                columns(at, at)
-                return carry
-
-            lax.fori_loop(0, 2, step, 0)
-        else:
-            columns(2 * tile, 0)
-
+def block_starts(place_ref, offsets, depth):
+    z, g = place_ref[0], place_ref[1]
+    return [
+        pl.multiple_of((((z + off) % RING) * GROUP + (g ^ j)) * depth, depth) for off in offsets for j in range(GROUP)
+    ]
+
+
+def contract(tok, starts, wts, first_column, tile, depth):
+    rows = [(w, row) for w in wts for row in range(0, w.shape[0], depth)]
+    raw = None
+    for start, (w, row) in zip(starts, rows, strict=True):
+        lhs = jnp.concatenate([t[:, pl.ds(start, depth)] for t in tok], axis=0)
+        part = jnp.dot(lhs, w[row : row + depth, pl.ds(first_column, tile)], preferred_element_type=jnp.float32)
+        raw = part if raw is None else raw + part
+    return raw
+
+
+def put(out_ref, column, raw, c, s, turn_second):
+    first, second = raw[:, :HEAD], raw[:, HEAD:]
+    out_ref[:, column : column + HEAD] = turned(first, c, s)
+    out_ref[:, column + HEAD : column + 2 * HEAD] = turned(second, c, s) if turn_second else second.astype(jnp.bfloat16)
+
+
+def cost(rows, depth, columns):
+    return pl.CostEstimate(
+        flops=2 * rows * depth * columns, transcendentals=0, bytes_accessed=2 * (rows * depth + depth * columns)
+    )
+
+
+def vmem_call(kernel, n_in, out_shape, limit, estimate, **more):
     vmem = pl.BlockSpec(memory_space=pltpu.VMEM)
     return pl.pallas_call(
         kernel,
-        in_specs=[pl.BlockSpec(memory_space=pltpu.SMEM)] + [vmem] * (len(tokens) + len(flat) + 2),
-        out_specs=vmem,
-        out_shape=jax.ShapeDtypeStruct((rows, out_width), jnp.bfloat16),
-        compiler_params=pltpu.CompilerParams(vmem_limit_bytes=PROJECT_VMEM),
-        cost_estimate=pl.CostEstimate(
-            flops=2 * rows * width * out_width, transcendentals=0, bytes_accessed=2 * (rows * width + width * out_width)
-        ),
-    )(place, *tokens, *flat, cos_table, sin_table)
+        in_specs=[pl.BlockSpec(memory_space=pltpu.SMEM)] + [vmem] * n_in,
+        out_specs=jax.tree.map(lambda _: vmem, out_shape),
+        out_shape=out_shape,
+        compiler_params=pltpu.CompilerParams(vmem_limit_bytes=limit << 20),
+        cost_estimate=estimate,
+        **more,
+    )
+
+
+def project_most(place, tokens, slabs, offsets):
+    rows = sum(t.shape[0] for t in tokens)
+    flat = [w for slab in slabs for w in slab]
+    depth = tokens[0].shape[1] // (RING * GROUP)
+    held, columns = sum(w.shape[0] for w in flat), flat[0].shape[1]
+    tile = 2 * HEAD
+
+    def kernel(place_ref, *refs):
+        tok, wts = refs[: len(tokens)], refs[len(tokens) : len(tokens) + len(flat)]
+        raw_ref, kept_ref = refs[len(tokens) + len(flat) :]
+        starts = block_starts(place_ref, offsets, depth)
+
+        def step(n, carry):
+            at = pl.multiple_of(n * tile, tile)
+            raw_ref[:, pl.ds(at, tile)] = contract(tok, starts, wts, at, tile, depth)
+            return carry
+
+        lax.fori_loop(0, columns // tile, step, 0)
+        at = 0
+        for w in wts:
+            kept_ref[at : at + w.shape[0]] = w[...]
+            at += w.shape[0]
+
+    out_shape = [
+        jax.ShapeDtypeStruct((rows, columns), jnp.float32),
+        jax.ShapeDtypeStruct((held, columns), jnp.bfloat16),
+    ]
+    return vmem_call(kernel, len(tokens) + len(flat), out_shape, 16, cost(rows, held, columns))(place, *tokens, *flat)
+
+
+def project_rest(place, tokens, raw, slab, offset, tables, queries):
+    rows = raw.shape[0]
+    depth = tokens[0].shape[1] // (RING * GROUP)
+    tile = 2 * HEAD
+    first, width = (0, 2 * tile) if queries else (2 * tile, tile)
+
+    def kernel(place_ref, *refs):
+        tok, wts = refs[: len(tokens)], refs[len(tokens) : len(tokens) + len(slab)]
+        raw_ref, cos_ref, sin_ref, out_ref = refs[len(tokens) + len(slab) :]
+        starts = block_starts(place_ref, [offset], depth)
+        for at in range(0, width, tile):
+            total = contract(tok, starts, wts, first + at, tile, depth) + raw_ref[:, first + at : first + at + tile]
+            put(out_ref, at, total, cos_ref[...], sin_ref[...], queries)
+
+    out_shape = jax.ShapeDtypeStruct((rows, width), jnp.bfloat16)
+    return vmem_call(kernel, len(tokens) + len(slab) + 3, out_shape, 8, cost(rows, 4 * depth, width))(
+        place, *tokens, *slab, raw, *tables
+    )
+
+
+def project_late(place, tokens, wts, offsets, tables):
+    rows = sum(t.shape[0] for t in tokens)
+    depth = tokens[0].shape[1] // (RING * GROUP)
+    tile = 2 * HEAD
+
+    def kernel(place_ref, *refs):
+        tok, weights = refs[: len(tokens)], refs[len(tokens) : len(tokens) + len(wts)]
+        cos_ref, sin_ref, kv_ref, q_ref = refs[len(tokens) + len(wts) :]
+        starts = block_starts(place_ref, offsets, depth)
+        for n in range(3):
+            raw = contract(tok, starts, weights, n * tile, tile, depth)
+            put(q_ref if n < 2 else kv_ref, n % 2 * tile, raw, cos_ref[...], sin_ref[...], n < 2)
+
+    out_shape = [
+        jax.ShapeDtypeStruct((rows, tile), jnp.bfloat16),
+        jax.ShapeDtypeStruct((rows, 2 * tile), jnp.bfloat16),
+    ]
+    return vmem_call(kernel, len(tokens) + len(wts) + 2, out_shape, 8, cost(rows, 16 * depth, 3 * tile))(
+        place, *tokens, *wts, *tables
+    )
 
 
 def best_of(s):
@@ -228,8 +268,8 @@
         v = values_and_ones(kv)
         for h in range(heads):
             mine = slice(h * rows, (h + 1) * rows)
-            old = tops_ref[piece, :, h * HEAD : h * HEAD + 1]
-            found, top, at = [], tops_ref[piece, :, h * HEAD : (h + 1) * HEAD], 0
+            old = tops_ref[piece, :, h * HEAD : (h + 1) * HEAD]
+            found, top, at = [], old, 0
             for d, slab in enumerate(below, start=1):
                 n = sum(p.shape[0] for p in slab)
                 s = s_ref[mine, at : at + n]
@@ -238,8 +278,11 @@
                 top = jnp.maximum(top, jnp.where(z >= d, best_of(s), NEG))
             top = jnp.max(top, axis=1, keepdims=True)
             mixed = weigh([(s, jnp.where(visible, top, -NEG)) for s, visible in found], v)
-            mixed = mixed + sums_ref[piece, :, 2 * h * HEAD : 2 * (h + 1) * HEAD] * jnp.exp2((old - top) * LOG2E_SCALE)
-            out_ref[:, h * HEAD : (h + 1) * HEAD] = (mixed[:, :HEAD] / mixed[:, HEAD:]).astype(jnp.bfloat16)
+            shrink = jnp.exp2((old - top) * LOG2E_SCALE)
+            at = 2 * h * HEAD
+            above = mixed[:, :HEAD] + sums_ref[piece, :, at : at + HEAD] * shrink
+            under = mixed[:, HEAD:] + sums_ref[piece, :, at + HEAD : at + 2 * HEAD] * shrink
+            out_ref[:, h * HEAD : (h + 1) * HEAD] = (above / under).astype(jnp.bfloat16)
 
     vmem = pl.BlockSpec(memory_space=pltpu.VMEM)
     return pl.pallas_call(
@@ -278,7 +321,8 @@
     other_right = along(other, -1)
     chip_far = along(chip_left, 1)
     other_far = along(other_right, -1)
-    weights = [[chip, other], [chip_right, other_right], [chip_far, other_far], [chip_left, other_left]]
+    most = [[chip, other], [chip_right, other_right], [chip_left, other_left]]
+    far = [chip_far, other_far]
 
     normed = normalize(tokens[0], norm_gain[0])
     side = near(normed, 1)
@@ -292,22 +336,16 @@
     late = [(2, half, half), (3, half, half)]
     tables_early = rope_tables(z, g, rows, early)
     tables_late = rope_tables(z, g, rows, late)
-    chunks_early = [[normed, side, across[0], corner[0]]]
-    chunks_late = [[across[1], corner[1]]]
-    kv_early = project(place, chunks_early, weights, *tables_early, False)
-    q_early = project(place, chunks_early, weights, *tables_early, True)
-    kv_late = project(place, chunks_late, weights, *tables_late, False)
-    q_late = project(place, chunks_late, weights, *tables_late, True)
-
-    cut = kv_early.shape[0] // 2
-    one = upward(kv_early, [(0, 1), (1, 2), (2, 3)])
-    three = upward(kv_early, [(0, 3), (1, 0)])
-    two_a = upward(one[:cut], [(1, 2), (2, 3)])
-    two_b = upward(three[cut:], [(3, 2), (0, 3)])
-    late_one = upward(kv_late, [(0, 1), (1, 2), (2, 3)])
-    late_two = upward(kv_late, [(0, 2), (1, 3)])
-    late_three = upward(kv_late, [(0, 3)])
-    below = [[one, late_one], [two_a, two_b, late_two], [three, late_three]]
+    tokens_early = [normed, side, across[0], corner[0]]
+    raw, kept = project_most(place, tokens_early, most, (0, 1, 3))
+    kv_early = project_rest(place, tokens_early, raw, far, 2, tables_early, False)
+    q_early = project_rest(place, tokens_early, raw, far, 2, tables_early, True)
+    kv_late, q_late = project_late(place, [across[1], corner[1]], [kept, *far], (0, 1, 3, 2), tables_late)
+
+    below = [[], [], []]
+    for kv in (kv_early, kv_late):
+        for d in (1, 2, 3):
+            below[d - 1].append(upward(kv, [(z0, z0 + d) for z0 in range(RING - d)]))
 
     sums, tops, queries = attend_own(place, q_early, q_late, kv_early, kv_late, early + late)
     out = jnp.zeros((rows, GROUP * GROUP * HEAD), jnp.bfloat16)

time: 212 us -> 179 us (0.84)
  waiting for transfers between devices: 114 us -> 85.9 us
  Pallas kernels: 47.3 us -> 43.7 us
  local copies, waits for them, and re-layouts: 5.1 us -> 7.37 us
    ppermute x6, waiting for transfers between devices: 49.7 us -> 24.2 us  [along(): lax.ppermute(block, 'seq', [(r, (r + step * GROUP) % n) for r in range(n)])]
    ppermute x8, waiting for transfers between devices: 57.3 us -> 48.1 us  [near(): lax.ppermute(block, 'seq', [(r, r ^ bits) for r in range(RING * GROUP)])]
    ppermute x6, starting transfers between devices: 9.36 us -> 13.4 us  [along(): lax.ppermute(block, 'seq', [(r, (r + step * GROUP) % n) for r in range(n)])]
    ppermute x7 -> x6, waiting for transfers between devices: 0.02 us -> 3.83 us  [upward(): lax.ppermute(block, 'seq', [(a * GROUP + g, b * GROUP + g) for a, b in ro...]
    pallas_call x4, Pallas kernels: 19.7 us -> 16.4 us  [the longest x1 7.49 us: project_most(): vmem_call(kernel, len(tokens) + len(flat), out_shape, 16, cost(rows, held...]
    ppermute x4, waiting for transfers between devices: 6.85 us -> 9.82 us  [onward(): return lax.ppermute(block, ('section', 'seq'), route)]
    ppermute x7 -> x6, starting transfers between devices: 14.3 us -> 11.6 us  [upward(): lax.ppermute(block, 'seq', [(a * GROUP + g, b * GROUP + g) for a, b in ro...]
    unnamed x11 -> x19, local copies, waits for them, and re-layouts: 1.67 us -> 3.99 us
  transfers between devices with their start and end apart: 25 -> 24, of which waited for: 8 -> 9; matrix products, arithmetic and copies ran while one was open for 2% -> 4% of each run, Pallas kernels for 20% -> 20%
where the time goes in v1:
time: 179 us; the launch traced here: 178 us
  waiting for transfers between devices  85.9 us (48%)
  Pallas kernels  43.7 us (24%)
  starting transfers between devices  36.6 us (20%)
  local copies, waits for them, and re-layouts  7.37 us (4%)
  other arithmetic  4.4 us (2%)
    ppermute x8, waiting for transfers between devices, near(): lax.ppermute(block, 'seq', [(r, r ^ bits) for r in range(RING * GROUP)])  48.1 us
    ppermute x6, waiting for transfers between devices, along(): lax.ppermute(block, 'seq', [(r, (r + step * GROUP) % n) for r in range(n)])  24.2 us
    pallas_call x4, Pallas kernels, attend_below(): pl.pallas_call(kernel, in_specs=[pl.BlockSpec(memory_space=pltpu.SMEM)] +...  19.9 us
    ppermute x6, starting transfers between devices, along(): lax.ppermute(block, 'seq', [(r, (r + step * GROUP) % n) for r in range(n)])  13.4 us
    ppermute x6, starting transfers between devices, upward(): lax.ppermute(block, 'seq', [(a * GROUP + g, b * GROUP + g) for a, b in ro...  11.6 us
    ppermute x4, waiting for transfers between devices, onward(): return lax.ppermute(block, ('section', 'seq'), route)  9.82 us
    pallas_call x1, Pallas kernels, project_most(): vmem_call(kernel, len(tokens) + len(flat), out_shape, 16, cost(rows, held...  7.49 us
    pallas_call x1, Pallas kernels, attend_own(): pl.pallas_call(kernel, grid=(GROUP,), in_specs=[pl.BlockSpec(memory_space...  7.35 us
  transfers between devices with their start and end apart: 24, of which 9 were waited for; matrix products, arithmetic and copies ran while one was open for 4% of the time, Pallas kernels for 20%

profile of v1, /device:TPU:0, one launch (start us, length us, event | category | flops | bytes accessed | tf_op | source)
XLA Modules:
  0.0 178.4 jit_solution(14175307759380156292)
XLA Ops:
  7.0 6.7 %collective-permute-done.6 = bf16[256,768]{1,0:T(8,128)(2,1)S(1)} collective-permute-done((bf16[256,768]{1,0:T(8,128)(2,1)S(1)}, bf16[256,768]{1,0:T(8,128)(2,1)S(1)}, u32[]{:S(2)}, u32[]{:S(2)}) %collective-permute-start.6) | collective-permute-done | bytes 393248 | tf_op jit(solution)/shard_map/ppermute | solution.py:19
  14.5 6.8 %collective-permute-done.7 = bf16[256,768]{1,0:T(8,128)(2,1)S(1)} collective-permute-done((bf16[256,768]{1,0:T(8,128)(2,1)S(1)}, bf16[256,768]{1,0:T(8,128)(2,1)S(1)}, u32[]{:S(2)}, u32[]{:S(2)}) %collective-permute-start.7) | collective-permute-done | bytes 393248 | tf_op jit(solution)/shard_map/ppermute | solution.py:19
  24.0 2.1 %collective-permute-start.8 = (bf16[512,768]{1,0:T(8,128)(2,1)}, bf16[512,768]{1,0:T(8,128)(2,1)}, u32[]{:S(2)}, u32[]{:S(2)}) collective-permute-start(bf16[512,768]{1,0:T(8,128)(2,1)} %constant_dynamic-update-slice_fusion.refs_5_), channel_id=1, source_target_pairs={{0,12},{1,13},{2,14},{3,15},{4,0},{5,1},{6,2},{7,3},{8,4},{9,5},{1... | collective-permute-start | bytes 2359304 | tf_op jit(solution)/shard_map/ppermute | solution.py:24
  27.1 17.4 %collective-permute-done.1.refs_2_ = bf16[128,4096]{1,0:T(8,128)(2,1)S(1)} collective-permute-done((bf16[128,4096]{1,0:T(8,128)(2,1)S(1)}, bf16[128,4096]{1,0:T(8,128)(2,1)S(1)}, u32[]{:S(2)}, u32[]{:S(2)}) %collective-permute-start.1) | collective-permute-done | bytes 1048608 | tf_op jit(solution)/shard_map/ppermute | solution.py:19
  44.6 4.2 %collective-permute-start.10 = (bf16[512,768]{1,0:T(8,128)(2,1)}, bf16[512,768]{1,0:T(8,128)(2,1)}, u32[]{:S(2)}, u32[]{:S(2)}) collective-permute-start(bf16[512,768]{1,0:T(8,128)(2,1)} %pad_maximum_fusion.refs_4_), channel_id=1, source_target_pairs={{0,12},{1,13},{2,14},{3,15},{4,0},{5,1},{6,2},{7,3},{8,4},{9,5},{1... | collective-permute-start | bytes 2359304 | tf_op jit(solution)/shard_map/ppermute | solution.py:24
  48.7 17.1 %collective-permute-done.12.refs_0_ = bf16[128,4096]{1,0:T(8,128)(2,1)S(1)} collective-permute-done((bf16[128,4096]{1,0:T(8,128)(2,1)S(1)}, bf16[128,4096]{1,0:T(8,128)(2,1)S(1)}, u32[]{:S(2)}, u32[]{:S(2)}) %collective-permute-start.12) | collective-permute-done | bytes 1048608 | tf_op jit(solution)/shard_map/ppermute | solution.py:19
  69.6 3.2 %collective-permute-start.9 = (bf16[512,768]{1,0:T(8,128)(2,1)}, bf16[512,768]{1,0:T(8,128)(2,1)S(1)}, u32[]{:S(2)}, u32[]{:S(2)}) collective-permute-start(bf16[512,768]{1,0:T(8,128)(2,1)} %collective-permute-done.8.refs_7_), channel_id=1, source_target_pairs={{0,12},{1,13},{2,14},{3,15},{4,0},{5,1},{6,2},{7,3},{8,4},{9,5},{1... | collective-permute-start | bytes 2359304 | tf_op jit(solution)/shard_map/ppermute | solution.py:24
  72.8 14.3 %collective-permute-done.4.refs_8_ = bf16[512,768]{1,0:T(8,128)(2,1)} collective-permute-done((bf16[512,768]{1,0:T(8,128)(2,1)}, bf16[512,768]{1,0:T(8,128)(2,1)}, u32[]{:S(2)}, u32[]{:S(2)}) %collective-permute-start.4) | collective-permute-done | bytes 786464 | tf_op jit(solution)/shard_map/ppermute | solution.py:24
  89.0 7.5 %shard_map.55 = (f32[768,768]{1,0:T(8,128)S(1)}, bf16[3072,768]{1,0:T(8,128)(2,1)S(1)}) custom-call(s32[2]{0:T(128)S(1)} %pad_add_fusion.place_ref, bf16[256,4096]{1,0:T(8,128)(2,1)S(1)} %fusion.2.refs_0_, bf16[256,4096]{1,0:T(8,128)(2,1)} %collective-permute-done.refs_1_, bf16[128,4096]{1,0:T(8,128)(2,1)S(1)} %collective-permute-done.1.refs_2_, ...), custom_call_target="tpu_custom_call" | custom-call | flops 3623878656 | bytes 9437184 | tf_op jit(solution)/shard_map/pallas_call | solution.py:127
  96.5 9.9 %collective-permute-done.5.refs_4_.refs_3_ = bf16[512,768]{1,0:T(8,128)(2,1)S(1)} collective-permute-done((bf16[512,768]{1,0:T(8,128)(2,1)}, bf16[512,768]{1,0:T(8,128)(2,1)S(1)}, u32[]{:S(2)}, u32[]{:S(2)}) %collective-permute-start.5) | collective-permute-done | bytes 786464 | tf_op jit(solution)/shard_map/ppermute | solution.py:24
  106.4 3.2 %shard_map.57 = (bf16[256,256]{1,0:T(8,128)(2,1)S(1)}, bf16[256,512]{1,0:T(8,128)(2,1)S(1)}) custom-call(s32[2]{0:T(128)S(1)} %pad_add_fusion.place_ref, bf16[128,4096]{1,0:T(8,128)(2,1)S(1)} %copy-done.1, bf16[128,4096]{1,0:T(8,128)(2,1)} %collective-permute-done.13.refs_1_, bf16[3072,768]{1,0:T(8,128)(2,1)S(1)} %get-tuple-element.13.refs_2_, ...), custom_call_target="tpu_custom_call" | custom-call | flops 1610612736 | bytes 8388608 | tf_op jit(solution)/shard_map/pallas_call | solution.py:167
  112.3 2.5 %shard_map.58.ke_ref = bf16[768,256]{1,0:T(8,128)(2,1)S(1)} custom-call(s32[2]{0:T(128)S(1)} %pad_add_fusion.place_ref, bf16[256,4096]{1,0:T(8,128)(2,1)S(1)} %fusion.2.refs_0_, bf16[256,4096]{1,0:T(8,128)(2,1)} %collective-permute-done.refs_1_, bf16[128,4096]{1,0:T(8,128)(2,1)S(1)} %collective-permute-done.1.refs_2_, ...), custom_call_target="tpu_custom_call" | custom-call | flops 402653184 | bytes 2097152 | tf_op jit(solution)/shard_map/pallas_call | solution.py:145
  114.9 2.6 %collective-permute-start.14 = (bf16[768,256]{1,0:T(8,128)(2,1)S(1)}, bf16[768,256]{1,0:T(8,128)(2,1)S(1)}, u32[]{:S(2)}, u32[]{:S(2)}) collective-permute-start(bf16[768,256]{1,0:T(8,128)(2,1)S(1)} %shard_map.58.ke_ref), channel_id=1, source_target_pairs={{0,4},{1,5},{2,6},{3,7},{4,8},{5,9},{6,10},{7,11},{8,12},{9,13},{1... | collective-permute-start | bytes 1179656 | tf_op jit(solution)/shard_map/ppermute | solution.py:28
  117.5 3.8 %collective-permute-start.16 = (bf16[768,256]{1,0:T(8,128)(2,1)S(1)}, bf16[768,256]{1,0:T(8,128)(2,1)S(1)}, u32[]{:S(2)}, u32[]{:S(2)}) collective-permute-start(bf16[768,256]{1,0:T(8,128)(2,1)S(1)} %shard_map.58.ke_ref), channel_id=1, source_target_pairs={{0,8},{1,9},{2,10},{3,11},{4,12},{5,13},{6,14},{7,15},{16,24},{17,... | collective-permute-start | bytes 1179656 | tf_op jit(solution)/shard_map/ppermute | solution.py:28
  123.9 3.2 %shard_map.56.qe_ref = bf16[768,512]{1,0:T(8,128)(2,1)S(1)} custom-call(s32[2]{0:T(128)S(1)} %pad_add_fusion.place_ref, bf16[256,4096]{1,0:T(8,128)(2,1)S(1)} %fusion.2.refs_0_, bf16[256,4096]{1,0:T(8,128)(2,1)} %collective-permute-done.refs_1_, bf16[128,4096]{1,0:T(8,128)(2,1)S(1)} %collective-permute-done.1.refs_2_, ...), custom_call_target="tpu_custom_call" | custom-call | flops 805306368 | bytes 2621440 | tf_op jit(solution)/shard_map/pallas_call | solution.py:145
  128.3 7.3 %shard_map.59 = (f32[4,256,1024]{2,1,0:T(8,128)S(1)}, f32[4,256,512]{2,1,0:T(8,128)S(1)}, bf16[1024,512]{1,0:T(8,128)(2,1)S(1)}) custom-call(s32[2]{0:T(128)S(1)} %pad_add_fusion.place_ref, bf16[768,512]{1,0:T(8,128)(2,1)S(1)} %shard_map.56.qe_ref, bf16[256,512]{1,0:T(8,128)(2,1)S(1)} %get-tuple-element.14.ql_ref, bf16[768,256]{1,0:T(8,128)(2,1)S(1)} %shard_map.58.ke_ref, ...), custom_call_target="tpu_custom_call" | custom-call | flops 4294967296 | bytes 3145728 | tf_op jit(solution)/shard_map/pallas_call | solution.py:235
  135.7 3.8 %collective-permute-done.19.refs_5_ = bf16[256,256]{1,0:T(8,128)(2,1)S(1)} collective-permute-done((bf16[256,256]{1,0:T(8,128)(2,1)S(1)}, bf16[256,256]{1,0:T(8,128)(2,1)S(1)}, u32[]{:S(2)}, u32[]{:S(2)}) %collective-permute-start.19) | collective-permute-done | bytes 131104 | tf_op jit(solution)/shard_map/ppermute | solution.py:28
  139.5 5.0 %shard_map.63 = bf16[256,512]{1,0:T(8,128)(2,1)S(1)} custom-call(s32[2]{0:T(128)S(1)} %pad_add_fusion.place_ref, f32[4,256,1024]{2,1,0:T(8,128)S(1)} %get-tuple-element.16.sums_ref, f32[4,256,512]{2,1,0:T(8,128)S(1)} %get-tuple-element.17.tops_ref, bf16[1024,512]{1,0:T(8,128)(2,1)S(1)} %get-tuple-element.18.q_ref, ...), custom_call_target="tpu_custom_call" | custom-call | flops 3221225472 | bytes 3145728 | tf_op jit(solution)/shard_map/pallas_call | solution.py:288
  144.5 2.4 %collective-permute-start.23 = (bf16[256,512]{1,0:T(8,128)(2,1)S(1)}, bf16[256,512]{1,0:T(8,128)(2,1)S(1)}, u32[]{:S(2)}, u32[]{:S(2)}) collective-permute-start(bf16[256,512]{1,0:T(8,128)(2,1)S(1)} %shard_map.63), channel_id=1, source_target_pairs={{0,19},{1,18},{2,17},{3,16},{4,23},{5,22},{6,21},{7,20},{8,27},{9,... | collective-permute-start | bytes 786440 | tf_op jit(solution)/shard_map/ppermute | solution.py:35
  146.9 5.0 %shard_map.61 = bf16[256,512]{1,0:T(8,128)(2,1)S(1)} custom-call(s32[2]{0:T(128)S(1)} %pad_add_fusion.place_ref, f32[4,256,1024]{2,1,0:T(8,128)S(1)} %get-tuple-element.16.sums_ref, f32[4,256,512]{2,1,0:T(8,128)S(1)} %get-tuple-element.17.tops_ref, bf16[1024,512]{1,0:T(8,128)(2,1)S(1)} %get-tuple-element.18.q_ref, ...), custom_call_target="tpu_custom_call" | custom-call | flops 3221225472 | bytes 3145728 | tf_op jit(solution)/shard_map/pallas_call | solution.py:288
  153.6 5.0 %shard_map.60 = bf16[256,512]{1,0:T(8,128)(2,1)S(1)} custom-call(s32[2]{0:T(128)S(1)} %pad_add_fusion.place_ref, f32[4,256,1024]{2,1,0:T(8,128)S(1)} %get-tuple-element.16.sums_ref, f32[4,256,512]{2,1,0:T(8,128)S(1)} %get-tuple-element.17.tops_ref, bf16[1024,512]{1,0:T(8,128)(2,1)S(1)} %get-tuple-element.18.q_ref, ...), custom_call_target="tpu_custom_call" | custom-call | flops 3221225472 | bytes 3145728 | tf_op jit(solution)/shard_map/pallas_call | solution.py:288
  160.1 5.0 %shard_map.62 = bf16[256,512]{1,0:T(8,128)(2,1)S(1)} custom-call(s32[2]{0:T(128)S(1)} %pad_add_fusion.place_ref, f32[4,256,1024]{2,1,0:T(8,128)S(1)} %get-tuple-element.16.sums_ref, f32[4,256,512]{2,1,0:T(8,128)S(1)} %get-tuple-element.17.tops_ref, bf16[1024,512]{1,0:T(8,128)(2,1)S(1)} %get-tuple-element.18.q_ref, ...), custom_call_target="tpu_custom_call" | custom-call | flops 3221225472 | bytes 3145728 | tf_op jit(solution)/shard_map/pallas_call | solution.py:288
  166.6 4.9 %collective-permute-done.20 = bf16[256,512]{1,0:T(8,128)(2,1)S(1)} collective-permute-done((bf16[256,512]{1,0:T(8,128)(2,1)S(1)}, bf16[256,512]{1,0:T(8,128)(2,1)S(1)}, u32[]{:S(2)}, u32[]{:S(2)}) %collective-permute-start.20) | collective-permute-done | bytes 262176 | tf_op jit(solution)/shard_map/ppermute | solution.py:35
  171.7 5.0 %collective-permute-done.22 = bf16[256,512]{1,0:T(8,128)(2,1)S(1)} collective-permute-done((bf16[256,512]{1,0:T(8,128)(2,1)S(1)}, bf16[256,512]{1,0:T(8,128)(2,1)S(1)}, u32[]{:S(2)}, u32[]{:S(2)}) %collective-permute-start.22) | collective-permute-done | bytes 262176 | tf_op jit(solution)/shard_map/ppermute | solution.py:35
  (79 shorter events, 30.2 us)
Async XLA Ops:
  1.6 12.1 %collective-permute-start.6 = (bf16[256,768]{1,0:T(8,128)(2,1)S(1)}, bf16[256,768]{1,0:T(8,128)(2,1)S(1)}, u32[]{:S(2)}, u32[]{:S(2)}) collective-permute-start(bf16[256,768]{1,0:T(8,128)(2,1)S(1)} %pad_maximum_fusion.2), channel_id=1, source_target_pairs={{0,2},{1,3},{2,0},{3,1},{4,6},{5,7},{6,4},{7,5},{8,10},{9,11},{10,... | collective-permute-start | bytes 1179656 | tf_op jit(solution)/shard_map/ppermute | solution.py:19
  3.4 17.9 %collective-permute-start.7 = (bf16[256,768]{1,0:T(8,128)(2,1)S(1)}, bf16[256,768]{1,0:T(8,128)(2,1)S(1)}, u32[]{:S(2)}, u32[]{:S(2)}) collective-permute-start(bf16[256,768]{1,0:T(8,128)(2,1)S(1)} %pad_maximum_fusion.3), channel_id=1, source_target_pairs={{0,3},{1,2},{2,1},{3,0},{4,7},{5,6},{6,5},{7,4},{8,11},{9,10},{10,... | collective-permute-start | bytes 1179656 | tf_op jit(solution)/shard_map/ppermute | solution.py:19
  4.9 39.7 %collective-permute-start.1 = (bf16[128,4096]{1,0:T(8,128)(2,1)S(1)}, bf16[128,4096]{1,0:T(8,128)(2,1)S(1)}, u32[]{:S(2)}, u32[]{:S(2)}) collective-permute-start(bf16[128,4096]{1,0:T(8,128)(2,1)S(1)} %get-tuple-element.20), channel_id=1, source_target_pairs={{0,2},{1,3},{2,0},{3,1},{4,6},{5,7},{6,4},{7,5},{8,10},{9,11},{10,... | collective-permute-start | bytes 3145736 | tf_op jit(solution)/shard_map/ppermute | solution.py:19
  6.1 59.8 %collective-permute-start.12 = (bf16[128,4096]{1,0:T(8,128)(2,1)S(1)}, bf16[128,4096]{1,0:T(8,128)(2,1)S(1)}, u32[]{:S(2)}, u32[]{:S(2)}) collective-permute-start(bf16[128,4096]{1,0:T(8,128)(2,1)S(1)} %get-tuple-element.19), channel_id=1, source_target_pairs={{0,2},{1,3},{2,0},{3,1},{4,6},{5,7},{6,4},{7,5},{8,10},{9,11},{10,... | collective-permute-start | bytes 3145736 | tf_op jit(solution)/shard_map/ppermute | solution.py:19
  7.0 80.8 %collective-permute-start = (bf16[256,4096]{1,0:T(8,128)(2,1)S(1)}, bf16[256,4096]{1,0:T(8,128)(2,1)}, u32[]{:S(2)}, u32[]{:S(2)}) collective-permute-start(bf16[256,4096]{1,0:T(8,128)(2,1)S(1)} %fusion.2.refs_0_), channel_id=1, source_target_pairs={{0,1},{1,0},{2,3},{3,2},{4,5},{5,4},{6,7},{7,6},{8,9},{9,8},{10,11... | collective-permute-start | bytes 6291464 | tf_op jit(solution)/shard_map/ppermute | solution.py:19
  13.7 10.4 %collective-permute-start.3 = (bf16[256,768]{1,0:T(8,128)(2,1)S(1)}, bf16[256,768]{1,0:T(8,128)(2,1)S(1)}, u32[]{:S(2)}, u32[]{:S(2)}) collective-permute-start(bf16[256,768]{1,0:T(8,128)(2,1)S(1)} %pad_maximum_fusion.1), channel_id=1, source_target_pairs={{0,1},{1,0},{2,3},{3,2},{4,5},{5,4},{6,7},{7,6},{8,9},{9,8},{10,11... | collective-permute-start | bytes 1179656 | tf_op jit(solution)/shard_map/ppermute | solution.py:19
  22.1 45.8 %collective-permute-start.11 = (bf16[512,768]{1,0:T(8,128)(2,1)}, bf16[512,768]{1,0:T(8,128)(2,1)S(1)}, u32[]{:S(2)}, u32[]{:S(2)}) collective-permute-start(bf16[512,768]{1,0:T(8,128)(2,1)} %constant_dynamic-update-slice_fusion.refs_5_), channel_id=1, source_target_pairs={{0,4},{1,5},{2,6},{3,7},{4,8},{5,9},{6,10},{7,11},{8,12},{9,13},{1... | collective-permute-start | bytes 2359304 | tf_op jit(solution)/shard_map/ppermute | solution.py:24
  24.0 45.0 %collective-permute-start.8 = (bf16[512,768]{1,0:T(8,128)(2,1)}, bf16[512,768]{1,0:T(8,128)(2,1)}, u32[]{:S(2)}, u32[]{:S(2)}) collective-permute-start(bf16[512,768]{1,0:T(8,128)(2,1)} %constant_dynamic-update-slice_fusion.refs_5_), channel_id=1, source_target_pairs={{0,12},{1,13},{2,14},{3,15},{4,0},{5,1},{6,2},{7,3},{8,4},{9,5},{1... | collective-permute-start | bytes 2359304 | tf_op jit(solution)/shard_map/ppermute | solution.py:24
  44.6 25.0 %collective-permute-start.10 = (bf16[512,768]{1,0:T(8,128)(2,1)}, bf16[512,768]{1,0:T(8,128)(2,1)}, u32[]{:S(2)}, u32[]{:S(2)}) collective-permute-start(bf16[512,768]{1,0:T(8,128)(2,1)} %pad_maximum_fusion.refs_4_), channel_id=1, source_target_pairs={{0,12},{1,13},{2,14},{3,15},{4,0},{5,1},{6,2},{7,3},{8,4},{9,5},{1... | collective-permute-start | bytes 2359304 | tf_op jit(solution)/shard_map/ppermute | solution.py:24
  65.9 21.2 %collective-permute-start.4 = (bf16[512,768]{1,0:T(8,128)(2,1)}, bf16[512,768]{1,0:T(8,128)(2,1)}, u32[]{:S(2)}, u32[]{:S(2)}) collective-permute-start(bf16[512,768]{1,0:T(8,128)(2,1)} %pad_maximum_fusion.refs_4_), channel_id=1, source_target_pairs={{0,4},{1,5},{2,6},{3,7},{4,8},{5,9},{6,10},{7,11},{8,12},{9,13},{1... | collective-permute-start | bytes 2359304 | tf_op jit(solution)/shard_map/ppermute | solution.py:24
  69.0 18.8 %collective-permute-start.2 = (bf16[128,4096]{1,0:T(8,128)(2,1)S(1)}, bf16[128,4096]{1,0:T(8,128)(2,1)}, u32[]{:S(2)}, u32[]{:S(2)}) collective-permute-start(bf16[128,4096]{1,0:T(8,128)(2,1)S(1)} %collective-permute-done.1.refs_2_), channel_id=1, source_target_pairs={{0,1},{1,0},{2,3},{3,2},{4,5},{5,4},{6,7},{7,6},{8,9},{9,8},{10,11... | collective-permute-start | bytes 3145736 | tf_op jit(solution)/shard_map/ppermute | solution.py:19
  69.1 37.3 %collective-permute-start.13 = (bf16[128,4096]{1,0:T(8,128)(2,1)}, bf16[128,4096]{1,0:T(8,128)(2,1)}, u32[]{:S(2)}, u32[]{:S(2)}) collective-permute-start(bf16[128,4096]{1,0:T(8,128)(2,1)} %copy-done), channel_id=1, source_target_pairs={{0,1},{1,0},{2,3},{3,2},{4,5},{5,4},{6,7},{7,6},{8,9},{9,8},{10,11... | collective-permute-start | bytes 3145736 | tf_op jit(solution)/shard_map/ppermute | solution.py:19
  69.6 26.8 %collective-permute-start.9 = (bf16[512,768]{1,0:T(8,128)(2,1)}, bf16[512,768]{1,0:T(8,128)(2,1)S(1)}, u32[]{:S(2)}, u32[]{:S(2)}) collective-permute-start(bf16[512,768]{1,0:T(8,128)(2,1)} %collective-permute-done.8.refs_7_), channel_id=1, source_target_pairs={{0,12},{1,13},{2,14},{3,15},{4,0},{5,1},{6,2},{7,3},{8,4},{9,5},{1... | collective-permute-start | bytes 2359304 | tf_op jit(solution)/shard_map/ppermute | solution.py:24
  87.1 19.3 %collective-permute-start.5 = (bf16[512,768]{1,0:T(8,128)(2,1)}, bf16[512,768]{1,0:T(8,128)(2,1)S(1)}, u32[]{:S(2)}, u32[]{:S(2)}) collective-permute-start(bf16[512,768]{1,0:T(8,128)(2,1)} %collective-permute-done.4.refs_8_), channel_id=1, source_target_pairs={{0,4},{1,5},{2,6},{3,7},{4,8},{5,9},{6,10},{7,11},{8,12},{9,13},{1... | collective-permute-start | bytes 2359304 | tf_op jit(solution)/shard_map/ppermute | solution.py:24
  109.6 17.5 %collective-permute-start.15 = (bf16[256,256]{1,0:T(8,128)(2,1)S(1)}, bf16[256,256]{1,0:T(8,128)(2,1)S(1)}, u32[]{:S(2)}, u32[]{:S(2)}) collective-permute-start(bf16[256,256]{1,0:T(8,128)(2,1)S(1)} %get-tuple-element.15.kl_ref), channel_id=1, source_target_pairs={{0,4},{1,5},{2,6},{3,7},{4,8},{5,9},{6,10},{7,11},{8,12},{9,13},{1... | collective-permute-start | bytes 393224 | tf_op jit(solution)/shard_map/ppermute | solution.py:28
  114.9 24.7 %collective-permute-start.14 = (bf16[768,256]{1,0:T(8,128)(2,1)S(1)}, bf16[768,256]{1,0:T(8,128)(2,1)S(1)}, u32[]{:S(2)}, u32[]{:S(2)}) collective-permute-start(bf16[768,256]{1,0:T(8,128)(2,1)S(1)} %shard_map.58.ke_ref), channel_id=1, source_target_pairs={{0,4},{1,5},{2,6},{3,7},{4,8},{5,9},{6,10},{7,11},{8,12},{9,13},{1... | collective-permute-start | bytes 1179656 | tf_op jit(solution)/shard_map/ppermute | solution.py:28
  117.5 22.1 %collective-permute-start.16 = (bf16[768,256]{1,0:T(8,128)(2,1)S(1)}, bf16[768,256]{1,0:T(8,128)(2,1)S(1)}, u32[]{:S(2)}, u32[]{:S(2)}) collective-permute-start(bf16[768,256]{1,0:T(8,128)(2,1)S(1)} %shard_map.58.ke_ref), channel_id=1, source_target_pairs={{0,8},{1,9},{2,10},{3,11},{4,12},{5,13},{6,14},{7,15},{16,24},{17,... | collective-permute-start | bytes 1179656 | tf_op jit(solution)/shard_map/ppermute | solution.py:28
  121.2 18.3 %collective-permute-start.18 = (bf16[768,256]{1,0:T(8,128)(2,1)S(1)}, bf16[768,256]{1,0:T(8,128)(2,1)S(1)}, u32[]{:S(2)}, u32[]{:S(2)}) collective-permute-start(bf16[768,256]{1,0:T(8,128)(2,1)S(1)} %shard_map.58.ke_ref), channel_id=1, source_target_pairs={{0,12},{1,13},{2,14},{3,15},{16,28},{17,29},{18,30},{19,31},{32,44... | collective-permute-start | bytes 1179656 | tf_op jit(solution)/shard_map/ppermute | solution.py:28
  122.5 13.1 %collective-permute-start.17 = (bf16[256,256]{1,0:T(8,128)(2,1)S(1)}, bf16[256,256]{1,0:T(8,128)(2,1)S(1)}, u32[]{:S(2)}, u32[]{:S(2)}) collective-permute-start(bf16[256,256]{1,0:T(8,128)(2,1)S(1)} %get-tuple-element.15.kl_ref), channel_id=1, source_target_pairs={{0,8},{1,9},{2,10},{3,11},{4,12},{5,13},{6,14},{7,15},{16,24},{17,... | collective-permute-start | bytes 393224 | tf_op jit(solution)/shard_map/ppermute | solution.py:28
  127.0 12.5 %collective-permute-start.19 = (bf16[256,256]{1,0:T(8,128)(2,1)S(1)}, bf16[256,256]{1,0:T(8,128)(2,1)S(1)}, u32[]{:S(2)}, u32[]{:S(2)}) collective-permute-start(bf16[256,256]{1,0:T(8,128)(2,1)S(1)} %get-tuple-element.15.kl_ref), channel_id=1, source_target_pairs={{0,12},{1,13},{2,14},{3,15},{16,28},{17,29},{18,30},{19,31},{32,44... | collective-permute-start | bytes 393224 | tf_op jit(solution)/shard_map/ppermute | solution.py:28
  144.5 32.2 %collective-permute-start.23 = (bf16[256,512]{1,0:T(8,128)(2,1)S(1)}, bf16[256,512]{1,0:T(8,128)(2,1)S(1)}, u32[]{:S(2)}, u32[]{:S(2)}) collective-permute-start(bf16[256,512]{1,0:T(8,128)(2,1)S(1)} %shard_map.63), channel_id=1, source_target_pairs={{0,19},{1,18},{2,17},{3,16},{4,23},{5,22},{6,21},{7,20},{8,27},{9,... | collective-permute-start | bytes 786440 | tf_op jit(solution)/shard_map/ppermute | solution.py:35
  151.9 19.8 %collective-permute-start.21 = (bf16[256,512]{1,0:T(8,128)(2,1)S(1)}, bf16[256,512]{1,0:T(8,128)(2,1)S(1)}, u32[]{:S(2)}, u32[]{:S(2)}) collective-permute-start(bf16[256,512]{1,0:T(8,128)(2,1)S(1)} %shard_map.61), channel_id=1, source_target_pairs={{0,17},{1,16},{2,19},{3,18},{4,21},{5,20},{6,23},{7,22},{8,25},{9,... | collective-permute-start | bytes 786440 | tf_op jit(solution)/shard_map/ppermute | solution.py:35
  158.6 12.9 %collective-permute-start.20 = (bf16[256,512]{1,0:T(8,128)(2,1)S(1)}, bf16[256,512]{1,0:T(8,128)(2,1)S(1)}, u32[]{:S(2)}, u32[]{:S(2)}) collective-permute-start(bf16[256,512]{1,0:T(8,128)(2,1)S(1)} %shard_map.60), channel_id=1, source_target_pairs={{0,16},{1,17},{2,18},{3,19},{4,20},{5,21},{6,22},{7,23},{8,24},{9,... | collective-permute-start | bytes 786440 | tf_op jit(solution)/shard_map/ppermute | solution.py:35
  165.1 11.6 %collective-permute-start.22 = (bf16[256,512]{1,0:T(8,128)(2,1)S(1)}, bf16[256,512]{1,0:T(8,128)(2,1)S(1)}, u32[]{:S(2)}, u32[]{:S(2)}) collective-permute-start(bf16[256,512]{1,0:T(8,128)(2,1)S(1)} %shard_map.62), channel_id=1, source_target_pairs={{0,18},{1,19},{2,16},{3,17},{4,22},{5,23},{6,20},{7,21},{8,26},{9,... | collective-permute-start | bytes 786440 | tf_op jit(solution)/shard_map/ppermute | solution.py:35
  (9 other events, 33.9 us)

commit v2 on v1

--- a/solution.py
+++ b/solution.py
@@ -35,10 +35,34 @@
     return lax.ppermute(block, ("section", "seq"), route)
 
 
-def normalize(rows_in, gain_row):
-    wide = rows_in.astype(jnp.float32)
-    scale = lax.rsqrt(jnp.mean(wide * wide, axis=-1, keepdims=True) + 1e-05)
-    return (wide * scale * gain_row.astype(jnp.float32)).astype(jnp.bfloat16)
+def normalize(tokens, gain_row):
+    rows, width = tokens.shape
+    step_rows, half = 32, rows // 2
+
+    def kernel(x_ref, gain_ref, whole_ref, low_ref, high_ref):
+        gain = gain_ref[...].astype(jnp.float32)
+
+        def step(i, carry):
+            mine = pl.ds(pl.multiple_of(i * step_rows, step_rows), step_rows)
+            wide = x_ref[mine].astype(jnp.float32)
+            scale = lax.rsqrt(jnp.mean(wide * wide, axis=-1, keepdims=True) + 1e-05)
+            whole_ref[mine] = (wide * scale * gain).astype(jnp.bfloat16)
+            return carry
+
+        lax.fori_loop(0, rows // step_rows, step, 0)
+        low_ref[...] = whole_ref[:half]
+        high_ref[...] = whole_ref[half:]
+
+    vmem = pl.BlockSpec(memory_space=pltpu.VMEM)
+    part = jax.ShapeDtypeStruct((half, width), jnp.bfloat16)
+    return pl.pallas_call(
+        kernel,
+        in_specs=[vmem, vmem],
+        out_specs=[vmem] * 3,
+        out_shape=[jax.ShapeDtypeStruct((rows, width), jnp.bfloat16), part, part],
+        compiler_params=pltpu.CompilerParams(vmem_limit_bytes=12 << 20),
+        cost_estimate=pl.CostEstimate(flops=4 * rows * width, transcendentals=rows, bytes_accessed=6 * rows * width),
+    )(tokens, gain_row)
 
 
 def rope_tables(z, g, rows, pieces):
@@ -62,20 +86,20 @@
     ]
 
 
-def contract(tok, starts, wts, first_column, tile, depth):
-    rows = [(w, row) for w in wts for row in range(0, w.shape[0], depth)]
+def contract(tok, starts, wts, column, tile, depth):
+    rows = [(w, base, row) for w, base in wts for row in range(0, w.shape[0], depth)]
     raw = None
-    for start, (w, row) in zip(starts, rows, strict=True):
+    for start, (w, base, row) in zip(starts, rows, strict=True):
         lhs = jnp.concatenate([t[:, pl.ds(start, depth)] for t in tok], axis=0)
-        part = jnp.dot(lhs, w[row : row + depth, pl.ds(first_column, tile)], preferred_element_type=jnp.float32)
+        part = jnp.dot(lhs, w[row : row + depth, pl.ds(base + column, tile)], preferred_element_type=jnp.float32)
         raw = part if raw is None else raw + part
     return raw
 
 
 def put(out_ref, column, raw, c, s, turn_second):
     first, second = raw[:, :HEAD], raw[:, HEAD:]
-    out_ref[:, column : column + HEAD] = turned(first, c, s)
-    out_ref[:, column + HEAD : column + 2 * HEAD] = turned(second, c, s) if turn_second else second.astype(jnp.bfloat16)
+    out_ref[:, pl.ds(column, HEAD)] = turned(first, c, s)
+    out_ref[:, pl.ds(column + HEAD, HEAD)] = turned(second, c, s) if turn_second else second.astype(jnp.bfloat16)
 
 
 def cost(rows, depth, columns):
@@ -97,75 +121,110 @@
     )
 
 
-def project_most(place, tokens, slabs, offsets):
+def pack(kept_ref, wts, width):
+    at = 0
+    for w, base in wts:
+        kept_ref[at : at + w.shape[0]] = w[:, base : base + width]
+        at += w.shape[0]
+
+
+def project_kv(place, tokens, wts, bases, offsets, tables):
     rows = sum(t.shape[0] for t in tokens)
-    flat = [w for slab in slabs for w in slab]
     depth = tokens[0].shape[1] // (RING * GROUP)
-    held, columns = sum(w.shape[0] for w in flat), flat[0].shape[1]
-    tile = 2 * HEAD
+    held, tile = sum(w.shape[0] for w in wts), 2 * HEAD
 
     def kernel(place_ref, *refs):
-        tok, wts = refs[: len(tokens)], refs[len(tokens) : len(tokens) + len(flat)]
-        raw_ref, kept_ref = refs[len(tokens) + len(flat) :]
+        tok, weights = refs[: len(tokens)], list(zip(refs[len(tokens) :], bases))
+        cos_ref, sin_ref, kv_ref, kept_ref = refs[len(tokens) + len(wts) :]
+        raw = contract(tok, block_starts(place_ref, offsets, depth), weights, 0, tile, depth)
+        put(kv_ref, 0, raw, cos_ref[:rows], sin_ref[:rows], False)
+        pack(kept_ref, weights, tile)
+
+    out_shape = [
+        jax.ShapeDtypeStruct((rows, tile), jnp.bfloat16),
+        jax.ShapeDtypeStruct((held, tile), jnp.bfloat16),
+    ]
+    return vmem_call(kernel, len(tokens) + len(wts) + 2, out_shape, 16, cost(rows, held, tile))(
+        place, *tokens, *wts, *tables
+    )
+
+
+def project_most(place, tokens, wts, offsets):
+    rows = sum(t.shape[0] for t in tokens)
+    depth = tokens[0].shape[1] // (RING * GROUP)
+    held, tile = sum(w.shape[0] for w in wts), 2 * HEAD
+
+    def kernel(place_ref, *refs):
+        tok, weights = refs[: len(tokens)], [(w, 0) for w in refs[len(tokens) : len(tokens) + len(wts)]]
+        raw_ref, kept_ref = refs[len(tokens) + len(wts) :]
         starts = block_starts(place_ref, offsets, depth)
 
         def step(n, carry):
             at = pl.multiple_of(n * tile, tile)
-            raw_ref[:, pl.ds(at, tile)] = contract(tok, starts, wts, at, tile, depth)
+            raw_ref[:, pl.ds(at, tile)] = contract(tok, starts, weights, at, tile, depth)
             return carry
 
-        lax.fori_loop(0, columns // tile, step, 0)
-        at = 0
-        for w in wts:
-            kept_ref[at : at + w.shape[0]] = w[...]
-            at += w.shape[0]
+        lax.fori_loop(0, 2, step, 0)
+        pack(kept_ref, weights, 2 * tile)
 
     out_shape = [
-        jax.ShapeDtypeStruct((rows, columns), jnp.float32),
-        jax.ShapeDtypeStruct((held, columns), jnp.bfloat16),
+        jax.ShapeDtypeStruct((rows, 2 * tile), jnp.float32),
+        jax.ShapeDtypeStruct((held, 2 * tile), jnp.bfloat16),
     ]
-    return vmem_call(kernel, len(tokens) + len(flat), out_shape, 16, cost(rows, held, columns))(place, *tokens, *flat)
-
-
-def project_rest(place, tokens, raw, slab, offset, tables, queries):
+    return vmem_call(kernel, len(tokens) + len(wts), out_shape, 16, cost(rows, held, 2 * tile))(place, *tokens, *wts)
+
+
+def project_rest(place, tokens, raw, slab, offset, tables):
     rows = raw.shape[0]
     depth = tokens[0].shape[1] // (RING * GROUP)
     tile = 2 * HEAD
-    first, width = (0, 2 * tile) if queries else (2 * tile, tile)
 
     def kernel(place_ref, *refs):
-        tok, wts = refs[: len(tokens)], refs[len(tokens) : len(tokens) + len(slab)]
+        tok, wts = refs[: len(tokens)], [(w, 0) for w in refs[len(tokens) : len(tokens) + len(slab)]]
         raw_ref, cos_ref, sin_ref, out_ref = refs[len(tokens) + len(slab) :]
         starts = block_starts(place_ref, [offset], depth)
-        for at in range(0, width, tile):
-            total = contract(tok, starts, wts, first + at, tile, depth) + raw_ref[:, first + at : first + at + tile]
-            put(out_ref, at, total, cos_ref[...], sin_ref[...], queries)
-
-    out_shape = jax.ShapeDtypeStruct((rows, width), jnp.bfloat16)
-    return vmem_call(kernel, len(tokens) + len(slab) + 3, out_shape, 8, cost(rows, 4 * depth, width))(
+
+        def step(n, carry):
+            at = pl.multiple_of(n * tile, tile)
+            total = contract(tok, starts, wts, at, tile, depth) + raw_ref[:, pl.ds(at, tile)]
+            put(out_ref, at, total, cos_ref[:rows], sin_ref[:rows], True)
+            return carry
+
+        lax.fori_loop(0, 2, step, 0)
+
+    out_shape = jax.ShapeDtypeStruct((rows, 2 * tile), jnp.bfloat16)
+    return vmem_call(kernel, len(tokens) + len(slab) + 3, out_shape, 8, cost(rows, 4 * depth, 2 * tile))(
         place, *tokens, *slab, raw, *tables
     )
 
 
-def project_late(place, tokens, wts, offsets, tables):
+def project_late(place, tokens, kv_weights, q_weights, offsets, tables):
     rows = sum(t.shape[0] for t in tokens)
     depth = tokens[0].shape[1] // (RING * GROUP)
     tile = 2 * HEAD
+    n, first = len(tokens), tables[0].shape[0] - rows
 
     def kernel(place_ref, *refs):
-        tok, weights = refs[: len(tokens)], refs[len(tokens) : len(tokens) + len(wts)]
-        cos_ref, sin_ref, kv_ref, q_ref = refs[len(tokens) + len(wts) :]
+        tok, kvw = refs[:n], [(refs[n], 0)]
+        qw = [(w, 0) for w in refs[n + 1 : n + 1 + len(q_weights)]]
+        cos_ref, sin_ref, kv_ref, q_ref = refs[n + 1 + len(q_weights) :]
         starts = block_starts(place_ref, offsets, depth)
-        for n in range(3):
-            raw = contract(tok, starts, weights, n * tile, tile, depth)
-            put(q_ref if n < 2 else kv_ref, n % 2 * tile, raw, cos_ref[...], sin_ref[...], n < 2)
+        raw = contract(tok, starts, kvw, 0, tile, depth)
+        put(kv_ref, 0, raw, cos_ref[first:], sin_ref[first:], False)
+
+        def step(n, carry):
+            at = pl.multiple_of(n * tile, tile)
+            put(q_ref, at, contract(tok, starts, qw, at, tile, depth), cos_ref[first:], sin_ref[first:], True)
+            return carry
+
+        lax.fori_loop(0, 2, step, 0)
 
     out_shape = [
         jax.ShapeDtypeStruct((rows, tile), jnp.bfloat16),
         jax.ShapeDtypeStruct((rows, 2 * tile), jnp.bfloat16),
     ]
-    return vmem_call(kernel, len(tokens) + len(wts) + 2, out_shape, 8, cost(rows, 16 * depth, 3 * tile))(
-        place, *tokens, *wts, *tables
+    return vmem_call(kernel, n + 1 + len(q_weights) + 2, out_shape, 8, cost(rows, 16 * depth, 3 * tile))(
+        place, *tokens, kv_weights, *q_weights, *tables
     )
 
 
@@ -313,38 +372,40 @@
     got = []
     for j in (1, 2, 3):
         got.append(near(columns(j), j))
+    nq = GROUP * HEAD
     chip = jnp.concatenate([columns(0), got[0]], axis=0)
-    other = jnp.concatenate([got[1], got[2]], axis=0)
-    chip_left = along(chip, 1)
-    chip_right = along(chip, -1)
-    other_left = along(other, 1)
-    other_right = along(other, -1)
-    chip_far = along(chip_left, 1)
-    other_far = along(other_right, -1)
-    most = [[chip, other], [chip_right, other_right], [chip_left, other_left]]
-    far = [chip_far, other_far]
-
-    normed = normalize(tokens[0], norm_gain[0])
+    other_kv = jnp.concatenate([got[1][:, nq:], got[2][:, nq:]], axis=0)
+    other_q = jnp.concatenate([got[1][:, :nq], got[2][:, :nq]], axis=0)
+
+    chip_left, chip_right = along(chip, 1), along(chip, -1)
+    kv_left, kv_right = along(other_kv, 1), along(other_kv, -1)
+    q_left, q_right = along(other_q, 1), along(other_q, -1)
+    chip_far, kv_far, q_far = along(chip_left, 1), along(kv_right, -1), along(q_right, -1)
+    offsets = (0, 1, 3, 2)
+    kv_weights = [chip, other_kv, chip_right, kv_right, chip_left, kv_left, chip_far, kv_far]
+    kv_bases = [nq, 0] * RING
+    q_weights = [chip, other_q, chip_right, q_right, chip_left, q_left]
+
+    normed, *halves = normalize(tokens[0], norm_gain)
     side = near(normed, 1)
     across, corner = [], []
     for i in range(2):
-        across.append(near(normed[i * half : (i + 1) * half], 2))
+        across.append(near(halves[i], 2))
     for i in range(2):
         corner.append(near(across[i], 1))
 
     early = [(0, 0, rows), (1, 0, rows), (2, 0, half), (3, 0, half)]
     late = [(2, half, half), (3, half, half)]
-    tables_early = rope_tables(z, g, rows, early)
-    tables_late = rope_tables(z, g, rows, late)
+    tables = rope_tables(z, g, rows, early + late)
     tokens_early = [normed, side, across[0], corner[0]]
-    raw, kept = project_most(place, tokens_early, most, (0, 1, 3))
-    kv_early = project_rest(place, tokens_early, raw, far, 2, tables_early, False)
-    q_early = project_rest(place, tokens_early, raw, far, 2, tables_early, True)
-    kv_late, q_late = project_late(place, [across[1], corner[1]], [kept, *far], (0, 1, 3, 2), tables_late)
+    kv_early, kept_kv = project_kv(place, tokens_early, kv_weights, kv_bases, offsets, tables)
+    raw, kept_q = project_most(place, tokens_early, q_weights, offsets[:3])
+    q_early = project_rest(place, tokens_early, raw, [chip_far, q_far], offsets[3], tables)
+    kv_late, q_late = project_late(place, [across[1], corner[1]], kept_kv, [kept_q, chip_far, q_far], offsets, tables)
 
     below = [[], [], []]
     for kv in (kv_early, kv_late):
-        for d in (1, 2, 3):
+        for d in (3, 2, 1):
             below[d - 1].append(upward(kv, [(z0, z0 + d) for z0 in range(RING - d)]))
 
     sums, tops, queries = attend_own(place, q_early, q_late, kv_early, kv_late, early + late)

time: 179 us -> 164 us (0.916)
  waiting for transfers between devices: 85.9 us -> 66.6 us
  Pallas kernels: 43.7 us -> 47.7 us
    ppermute x8, waiting for transfers between devices: 48.1 us -> 35.6 us  [near(): lax.ppermute(block, 'seq', [(r, r ^ bits) for r in range(RING * GROUP)])]
    pallas_call x2 -> x4, Pallas kernels: 10.7 us -> 17.1 us  [the longest x1 5.55 us: project_most(): vmem_call(kernel, len(tokens) + len(wts), out_shape, 16, cost(rows, held,...]
    ppermute x6 -> x9, waiting for transfers between devices: 24.2 us -> 18.1 us  [along(): lax.ppermute(block, 'seq', [(r, (r + step * GROUP) % n) for r in range(n)])]
    pallas_call x2 -> x1, Pallas kernels: 5.69 us -> 3.49 us  [project_rest(): vmem_call(kernel, len(tokens) + len(slab) + 3, out_shape, 8, cost(rows, 4...]
    unnamed x19 -> x30, local copies, waits for them, and re-layouts: 3.99 us -> 6.09 us
    ppermute x6 -> x9, starting transfers between devices: 13.4 us -> 14.1 us  [along(): lax.ppermute(block, 'seq', [(r, (r + step * GROUP) % n) for r in range(n)])]
  transfers between devices with their start and end apart: 24 -> 27, of which waited for: 9 -> 12; matrix products, arithmetic and copies ran while one was open for 4% -> 2% of each run, Pallas kernels for 20% -> 24%
where the time goes in v2:
time: 164 us
  waiting for transfers between devices  66.6 us (41%)
  Pallas kernels  47.7 us (29%)
  starting transfers between devices  37.2 us (23%)
  local copies, waits for them, and re-layouts  8.48 us (5%)
  other arithmetic  3.22 us (2%)
    ppermute x8, waiting for transfers between devices, near(): lax.ppermute(block, 'seq', [(r, r ^ bits) for r in range(RING * GROUP)])  35.6 us
    pallas_call x4, Pallas kernels, attend_below(): pl.pallas_call(kernel, in_specs=[pl.BlockSpec(memory_space=pltpu.SMEM)] +...  19.9 us
    ppermute x9, waiting for transfers between devices, along(): lax.ppermute(block, 'seq', [(r, (r + step * GROUP) % n) for r in range(n)])  18.1 us
    ppermute x9, starting transfers between devices, along(): lax.ppermute(block, 'seq', [(r, (r + step * GROUP) % n) for r in range(n)])  14.1 us
    ppermute x6, starting transfers between devices, upward(): lax.ppermute(block, 'seq', [(a * GROUP + g, b * GROUP + g) for a, b in ro...  10.4 us
    ppermute x4, waiting for transfers between devices, onward(): return lax.ppermute(block, ('section', 'seq'), route)  8.78 us
    pallas_call x1, Pallas kernels, attend_own(): pl.pallas_call(kernel, grid=(GROUP,), in_specs=[pl.BlockSpec(memory_space...  7.25 us
    ppermute x4, starting transfers between devices, onward(): return lax.ppermute(block, ('section', 'seq'), route)  6.94 us
  transfers between devices with their start and end apart: 27, of which 12 were waited for; matrix products, arithmetic and copies ran while one was open for 2% of the time, Pallas kernels for 24%

profile of v2, /device:TPU:0, one launch (start us, length us, event | category | flops | bytes accessed | tf_op | source)
XLA Modules:
  0.0 163.7 jit_solution(15982219773265790070)
XLA Ops:
  4.0 9.6 %collective-permute-done.6 = bf16[256,768]{1,0:T(8,128)(2,1)S(1)} collective-permute-done((bf16[256,768]{1,0:T(8,128)(2,1)S(1)}, bf16[256,768]{1,0:T(8,128)(2,1)S(1)}, u32[]{:S(2)}, u32[]{:S(2)}) %collective-permute-start.6) | collective-permute-done | bytes 393248 | tf_op jit(solution)/shard_map/ppermute | solution.py:19
  13.6 6.5 %collective-permute-done.7 = bf16[256,768]{1,0:T(8,128)(2,1)S(1)} collective-permute-done((bf16[256,768]{1,0:T(8,128)(2,1)S(1)}, bf16[256,768]{1,0:T(8,128)(2,1)S(1)}, u32[]{:S(2)}, u32[]{:S(2)}) %collective-permute-start.7) | collective-permute-done | bytes 393248 | tf_op jit(solution)/shard_map/ppermute | solution.py:19
  20.1 4.1 %collective-permute-start.14 = (bf16[512,256]{1,0:T(8,128)(2,1)S(1)}, bf16[512,256]{1,0:T(8,128)(2,1)S(1)}, u32[]{:S(2)}, u32[]{:S(2)}) collective-permute-start(bf16[512,256]{1,0:T(8,128)(2,1)S(1)} %pad_maximum_fusion.5.refs_5_), channel_id=1, source_target_pairs={{0,12},{1,13},{2,14},{3,15},{4,0},{5,1},{6,2},{7,3},{8,4},{9,5},{1... | collective-permute-start | bytes 786440 | tf_op jit(solution)/shard_map/ppermute | solution.py:24
  24.2 2.9 %shard_map.55 = (bf16[256,4096]{1,0:T(8,128)(2,1)S(1)}, bf16[128,4096]{1,0:T(8,128)(2,1)}, bf16[128,4096]{1,0:T(8,128)(2,1)}) custom-call(bf16[256,4096]{1,0:T(8,128)(2,1)S(1)} %bitcast.35, bf16[1,4096]{1,0:T(2,128)(2,1)S(1)} %copy-done.11), custom_call_target="tpu_custom_call" | custom-call | flops 4194304 | bytes 6291456 | tf_op jit(solution)/shard_map/pallas_call | solution.py:58
  30.7 3.7 %collective-permute-start.16 = (bf16[512,256]{1,0:T(8,128)(2,1)S(1)}, bf16[512,256]{1,0:T(8,128)(2,1)S(1)}, u32[]{:S(2)}, u32[]{:S(2)}) collective-permute-start(bf16[512,256]{1,0:T(8,128)(2,1)S(1)} %collective-permute-done.14.refs_7_), channel_id=1, source_target_pairs={{0,12},{1,13},{2,14},{3,15},{4,0},{5,1},{6,2},{7,3},{8,4},{9,5},{1... | collective-permute-start | bytes 786440 | tf_op jit(solution)/shard_map/ppermute | solution.py:24
  34.5 4.7 %collective-permute-done.15.refs_9_ = bf16[512,256]{1,0:T(8,128)(2,1)S(1)} collective-permute-done((bf16[512,256]{1,0:T(8,128)(2,1)S(1)}, bf16[512,256]{1,0:T(8,128)(2,1)S(1)}, u32[]{:S(2)}, u32[]{:S(2)}) %collective-permute-start.15) | collective-permute-done | bytes 262176 | tf_op jit(solution)/shard_map/ppermute | solution.py:24
  43.4 8.8 %collective-permute-done.8.refs_7_ = bf16[512,512]{1,0:T(8,128)(2,1)S(1)} collective-permute-done((bf16[512,512]{1,0:T(8,128)(2,1)S(1)}, bf16[512,512]{1,0:T(8,128)(2,1)S(1)}, u32[]{:S(2)}, u32[]{:S(2)}) %collective-permute-start.8) | collective-permute-done | bytes 524320 | tf_op jit(solution)/shard_map/ppermute | solution.py:24
  53.0 2.7 %collective-permute-start.10 = (bf16[512,768]{1,0:T(8,128)(2,1)}, bf16[512,768]{1,0:T(8,128)(2,1)}, u32[]{:S(2)}, u32[]{:S(2)}) collective-permute-start(bf16[512,768]{1,0:T(8,128)(2,1)} %pad_maximum_fusion.refs_4_), channel_id=1, source_target_pairs={{0,12},{1,13},{2,14},{3,15},{4,0},{5,1},{6,2},{7,3},{8,4},{9,5},{1... | collective-permute-start | bytes 2359304 | tf_op jit(solution)/shard_map/ppermute | solution.py:24
  55.9 19.5 %collective-permute-done.12.refs_0_ = bf16[128,4096]{1,0:T(8,128)(2,1)} collective-permute-done((bf16[128,4096]{1,0:T(8,128)(2,1)}, bf16[128,4096]{1,0:T(8,128)(2,1)}, u32[]{:S(2)}, u32[]{:S(2)}) %collective-permute-start.12) | collective-permute-done | bytes 1048608 | tf_op jit(solution)/shard_map/ppermute | solution.py:19
  75.6 3.4 %collective-permute-start.9 = (bf16[512,512]{1,0:T(8,128)(2,1)}, bf16[512,512]{1,0:T(8,128)(2,1)S(1)}, u32[]{:S(2)}, u32[]{:S(2)}) collective-permute-start(bf16[512,512]{1,0:T(8,128)(2,1)} %copy-done.3), channel_id=1, source_target_pairs={{0,12},{1,13},{2,14},{3,15},{4,0},{5,1},{6,2},{7,3},{8,4},{9,5},{1... | collective-permute-start | bytes 1572872 | tf_op jit(solution)/shard_map/ppermute | solution.py:24
  83.8 4.8 %shard_map.58 = (bf16[768,256]{1,0:T(8,128)(2,1)S(1)}, bf16[4096,256]{1,0:T(8,128)(2,1)S(1)}) custom-call(s32[2]{0:T(128)S(1)} %pad_add_fusion.place_ref, bf16[256,4096]{1,0:T(8,128)(2,1)S(1)} %get-tuple-element.17.refs_0_, bf16[256,4096]{1,0:T(8,128)(2,1)} %collective-permute-done.refs_1_, bf16[128,4096]{1,0:T(8,128)(2,1)S(1)} %collective-permute-done.1.refs_2_, ...), custom_call_target="tpu_custom_call" | custom-call | flops 1610612736 | bytes 8388608 | tf_op jit(solution)/shard_map/pallas_call | solution.py:147
  91.3 5.6 %shard_map.56 = (f32[768,512]{1,0:T(8,128)S(1)}, bf16[3072,512]{1,0:T(8,128)(2,1)S(1)}) custom-call(s32[2]{0:T(128)S(1)} %pad_add_fusion.place_ref, bf16[256,4096]{1,0:T(8,128)(2,1)S(1)} %get-tuple-element.17.refs_0_, bf16[256,4096]{1,0:T(8,128)(2,1)} %collective-permute-done.refs_1_, bf16[128,4096]{1,0:T(8,128)(2,1)S(1)} %collective-permute-done.1.refs_2_, ...), custom_call_target="tpu_custom_call" | custom-call | flops 2415919104 | bytes 7864320 | tf_op jit(solution)/shard_map/pallas_call | solution.py:174
  96.8 3.8 %shard_map.59 = (bf16[256,256]{1,0:T(8,128)(2,1)S(1)}, bf16[256,512]{1,0:T(8,128)(2,1)S(1)}) custom-call(s32[2]{0:T(128)S(1)} %pad_add_fusion.place_ref, bf16[128,4096]{1,0:T(8,128)(2,1)} %collective-permute-done.12.refs_0_, bf16[128,4096]{1,0:T(8,128)(2,1)S(1)} %collective-permute-done.13.refs_1_, bf16[4096,256]{1,0:T(8,128)(2,1)S(1)} %get-tuple-element.21.refs_2_, ...), custom_call_target="tpu_custom_call" | custom-call | flops 1610612736 | bytes 8388608 | tf_op jit(solution)/shard_map/pallas_call | solution.py:226
  102.0 3.6 %collective-permute-start.20 = (bf16[256,256]{1,0:T(8,128)(2,1)S(1)}, bf16[256,256]{1,0:T(8,128)(2,1)S(1)}, u32[]{:S(2)}, u32[]{:S(2)}) collective-permute-start(bf16[256,256]{1,0:T(8,128)(2,1)S(1)} %get-tuple-element.25.kl_ref), channel_id=1, source_target_pairs={{0,8},{1,9},{2,10},{3,11},{4,12},{5,13},{6,14},{7,15},{16,24},{17,... | collective-permute-start | bytes 393224 | tf_op jit(solution)/shard_map/ppermute | solution.py:28
  109.6 3.5 %shard_map.57.qe_ref = bf16[768,512]{1,0:T(8,128)(2,1)S(1)} custom-call(s32[2]{0:T(128)S(1)} %pad_add_fusion.place_ref, bf16[256,4096]{1,0:T(8,128)(2,1)S(1)} %get-tuple-element.17.refs_0_, bf16[256,4096]{1,0:T(8,128)(2,1)} %collective-permute-done.refs_1_, bf16[128,4096]{1,0:T(8,128)(2,1)S(1)} %collective-permute-done.1.refs_2_, ...), custom_call_target="tpu_custom_call" | custom-call | flops 805306368 | bytes 2621440 | tf_op jit(solution)/shard_map/pallas_call | solution.py:196
  114.6 7.3 %shard_map.60 = (f32[4,256,1024]{2,1,0:T(8,128)S(1)}, f32[4,256,512]{2,1,0:T(8,128)S(1)}, bf16[1024,512]{1,0:T(8,128)(2,1)S(1)}) custom-call(s32[2]{0:T(128)S(1)} %pad_add_fusion.place_ref, bf16[768,512]{1,0:T(8,128)(2,1)S(1)} %shard_map.57.qe_ref, bf16[256,512]{1,0:T(8,128)(2,1)S(1)} %get-tuple-element.23.ql_ref, ...), custom_call_target="tpu_custom_call" | custom-call | flops 4294967296 | bytes 3145728 | tf_op jit(solution)/shard_map/pallas_call | solution.py:294
  121.9 3.0 %collective-permute-done.19.refs_2_ = bf16[768,256]{1,0:T(8,128)(2,1)S(1)} collective-permute-done((bf16[768,256]{1,0:T(8,128)(2,1)S(1)}, bf16[768,256]{1,0:T(8,128)(2,1)S(1)}, u32[]{:S(2)}, u32[]{:S(2)}) %collective-permute-start.19) | collective-permute-done | bytes 393248 | tf_op jit(solution)/shard_map/ppermute | solution.py:28
  126.1 5.0 %shard_map.64 = bf16[256,512]{1,0:T(8,128)(2,1)S(1)} custom-call(s32[2]{0:T(128)S(1)} %pad_add_fusion.place_ref, f32[4,256,1024]{2,1,0:T(8,128)S(1)} %get-tuple-element.26.sums_ref, f32[4,256,512]{2,1,0:T(8,128)S(1)} %get-tuple-element.27.tops_ref, bf16[1024,512]{1,0:T(8,128)(2,1)S(1)} %get-tuple-element.28.q_ref, ...), custom_call_target="tpu_custom_call" | custom-call | flops 3221225472 | bytes 3145728 | tf_op jit(solution)/shard_map/pallas_call | solution.py:347
  132.0 5.0 %shard_map.62 = bf16[256,512]{1,0:T(8,128)(2,1)S(1)} custom-call(s32[2]{0:T(128)S(1)} %pad_add_fusion.place_ref, f32[4,256,1024]{2,1,0:T(8,128)S(1)} %get-tuple-element.26.sums_ref, f32[4,256,512]{2,1,0:T(8,128)S(1)} %get-tuple-element.27.tops_ref, bf16[1024,512]{1,0:T(8,128)(2,1)S(1)} %get-tuple-element.28.q_ref, ...), custom_call_target="tpu_custom_call" | custom-call | flops 3221225472 | bytes 3145728 | tf_op jit(solution)/shard_map/pallas_call | solution.py:347
  137.0 3.2 %collective-permute-start.24 = (bf16[256,512]{1,0:T(8,128)(2,1)S(1)}, bf16[256,512]{1,0:T(8,128)(2,1)S(1)}, u32[]{:S(2)}, u32[]{:S(2)}) collective-permute-start(bf16[256,512]{1,0:T(8,128)(2,1)S(1)} %shard_map.62), channel_id=1, source_target_pairs={{0,17},{1,16},{2,19},{3,18},{4,21},{5,20},{6,23},{7,22},{8,25},{9,... | collective-permute-start | bytes 786440 | tf_op jit(solution)/shard_map/ppermute | solution.py:35
  140.2 5.0 %shard_map.61 = bf16[256,512]{1,0:T(8,128)(2,1)S(1)} custom-call(s32[2]{0:T(128)S(1)} %pad_add_fusion.place_ref, f32[4,256,1024]{2,1,0:T(8,128)S(1)} %get-tuple-element.26.sums_ref, f32[4,256,512]{2,1,0:T(8,128)S(1)} %get-tuple-element.27.tops_ref, bf16[1024,512]{1,0:T(8,128)(2,1)S(1)} %get-tuple-element.28.q_ref, ...), custom_call_target="tpu_custom_call" | custom-call | flops 3221225472 | bytes 3145728 | tf_op jit(solution)/shard_map/pallas_call | solution.py:347
  146.4 5.0 %shard_map.63 = bf16[256,512]{1,0:T(8,128)(2,1)S(1)} custom-call(s32[2]{0:T(128)S(1)} %pad_add_fusion.place_ref, f32[4,256,1024]{2,1,0:T(8,128)S(1)} %get-tuple-element.26.sums_ref, f32[4,256,512]{2,1,0:T(8,128)S(1)} %get-tuple-element.27.tops_ref, bf16[1024,512]{1,0:T(8,128)(2,1)S(1)} %get-tuple-element.28.q_ref, ...), custom_call_target="tpu_custom_call" | custom-call | flops 3221225472 | bytes 3145728 | tf_op jit(solution)/shard_map/pallas_call | solution.py:347
  153.0 3.2 %collective-permute-done.23 = bf16[256,512]{1,0:T(8,128)(2,1)S(1)} collective-permute-done((bf16[256,512]{1,0:T(8,128)(2,1)S(1)}, bf16[256,512]{1,0:T(8,128)(2,1)S(1)}, u32[]{:S(2)}, u32[]{:S(2)}) %collective-permute-start.23) | collective-permute-done | bytes 262176 | tf_op jit(solution)/shard_map/ppermute | solution.py:35
  156.4 5.5 %collective-permute-done.25 = bf16[256,512]{1,0:T(8,128)(2,1)S(1)} collective-permute-done((bf16[256,512]{1,0:T(8,128)(2,1)S(1)}, bf16[256,512]{1,0:T(8,128)(2,1)S(1)}, u32[]{:S(2)}, u32[]{:S(2)}) %collective-permute-start.25) | collective-permute-done | bytes 262176 | tf_op jit(solution)/shard_map/ppermute | solution.py:35
  (99 shorter events, 33.8 us)
Async XLA Ops:
  1.5 12.1 %collective-permute-start.6 = (bf16[256,768]{1,0:T(8,128)(2,1)S(1)}, bf16[256,768]{1,0:T(8,128)(2,1)S(1)}, u32[]{:S(2)}, u32[]{:S(2)}) collective-permute-start(bf16[256,768]{1,0:T(8,128)(2,1)S(1)} %pad_maximum_fusion.3), channel_id=1, source_target_pairs={{0,2},{1,3},{2,0},{3,1},{4,6},{5,7},{6,4},{7,5},{8,10},{9,11},{10,... | collective-permute-start | bytes 1179656 | tf_op jit(solution)/shard_map/ppermute | solution.py:19
  3.3 16.8 %collective-permute-start.7 = (bf16[256,768]{1,0:T(8,128)(2,1)S(1)}, bf16[256,768]{1,0:T(8,128)(2,1)S(1)}, u32[]{:S(2)}, u32[]{:S(2)}) collective-permute-start(bf16[256,768]{1,0:T(8,128)(2,1)S(1)} %pad_maximum_fusion.4), channel_id=1, source_target_pairs={{0,3},{1,2},{2,1},{3,0},{4,7},{5,6},{6,5},{7,4},{8,11},{9,10},{10,... | collective-permute-start | bytes 1179656 | tf_op jit(solution)/shard_map/ppermute | solution.py:19
  3.5 25.4 %collective-permute-start.3 = (bf16[256,768]{1,0:T(8,128)(2,1)S(1)}, bf16[256,768]{1,0:T(8,128)(2,1)S(1)}, u32[]{:S(2)}, u32[]{:S(2)}) collective-permute-start(bf16[256,768]{1,0:T(8,128)(2,1)S(1)} %pad_maximum_fusion.2), channel_id=1, source_target_pairs={{0,1},{1,0},{2,3},{3,2},{4,5},{5,4},{6,7},{7,6},{8,9},{9,8},{10,11... | collective-permute-start | bytes 1179656 | tf_op jit(solution)/shard_map/ppermute | solution.py:19
  20.1 10.6 %collective-permute-start.14 = (bf16[512,256]{1,0:T(8,128)(2,1)S(1)}, bf16[512,256]{1,0:T(8,128)(2,1)S(1)}, u32[]{:S(2)}, u32[]{:S(2)}) collective-permute-start(bf16[512,256]{1,0:T(8,128)(2,1)S(1)} %pad_maximum_fusion.5.refs_5_), channel_id=1, source_target_pairs={{0,12},{1,13},{2,14},{3,15},{4,0},{5,1},{6,2},{7,3},{8,4},{9,5},{1... | collective-permute-start | bytes 786440 | tf_op jit(solution)/shard_map/ppermute | solution.py:24
  27.1 28.6 %collective-permute-start.1 = (bf16[128,4096]{1,0:T(8,128)(2,1)}, bf16[128,4096]{1,0:T(8,128)(2,1)S(1)}, u32[]{:S(2)}, u32[]{:S(2)}) collective-permute-start(bf16[128,4096]{1,0:T(8,128)(2,1)} %get-tuple-element.18), channel_id=1, source_target_pairs={{0,2},{1,3},{2,0},{3,1},{4,6},{5,7},{6,4},{7,5},{8,10},{9,11},{10,... | collective-permute-start | bytes 3145736 | tf_op jit(solution)/shard_map/ppermute | solution.py:19
  28.4 52.5 %collective-permute-start = (bf16[256,4096]{1,0:T(8,128)(2,1)S(1)}, bf16[256,4096]{1,0:T(8,128)(2,1)}, u32[]{:S(2)}, u32[]{:S(2)}) collective-permute-start(bf16[256,4096]{1,0:T(8,128)(2,1)S(1)} %get-tuple-element.17.refs_0_), channel_id=1, source_target_pairs={{0,1},{1,0},{2,3},{3,2},{4,5},{5,4},{6,7},{7,6},{8,9},{9,8},{10,11... | collective-permute-start | bytes 6291464 | tf_op jit(solution)/shard_map/ppermute | solution.py:19
  29.8 25.9 %collective-permute-start.4 = (bf16[512,768]{1,0:T(8,128)(2,1)}, bf16[512,768]{1,0:T(8,128)(2,1)}, u32[]{:S(2)}, u32[]{:S(2)}) collective-permute-start(bf16[512,768]{1,0:T(8,128)(2,1)} %pad_maximum_fusion.refs_4_), channel_id=1, source_target_pairs={{0,4},{1,5},{2,6},{3,7},{4,8},{5,9},{6,10},{7,11},{8,12},{9,13},{1... | collective-permute-start | bytes 2359304 | tf_op jit(solution)/shard_map/ppermute | solution.py:24
  40.0 12.2 %collective-permute-start.8 = (bf16[512,512]{1,0:T(8,128)(2,1)S(1)}, bf16[512,512]{1,0:T(8,128)(2,1)S(1)}, u32[]{:S(2)}, u32[]{:S(2)}) collective-permute-start(bf16[512,512]{1,0:T(8,128)(2,1)S(1)} %pad_maximum_fusion.1.refs_5_), channel_id=1, source_target_pairs={{0,12},{1,13},{2,14},{3,15},{4,0},{5,1},{6,2},{7,3},{8,4},{9,5},{1... | collective-permute-start | bytes 1572872 | tf_op jit(solution)/shard_map/ppermute | solution.py:24
  41.8 33.6 %collective-permute-start.12 = (bf16[128,4096]{1,0:T(8,128)(2,1)}, bf16[128,4096]{1,0:T(8,128)(2,1)}, u32[]{:S(2)}, u32[]{:S(2)}) collective-permute-start(bf16[128,4096]{1,0:T(8,128)(2,1)} %get-tuple-element.20), channel_id=1, source_target_pairs={{0,2},{1,3},{2,0},{3,1},{4,6},{5,7},{6,4},{7,5},{8,10},{9,11},{10,... | collective-permute-start | bytes 3145736 | tf_op jit(solution)/shard_map/ppermute | solution.py:19
  53.0 22.5 %collective-permute-start.10 = (bf16[512,768]{1,0:T(8,128)(2,1)}, bf16[512,768]{1,0:T(8,128)(2,1)}, u32[]{:S(2)}, u32[]{:S(2)}) collective-permute-start(bf16[512,768]{1,0:T(8,128)(2,1)} %pad_maximum_fusion.refs_4_), channel_id=1, source_target_pairs={{0,12},{1,13},{2,14},{3,15},{4,0},{5,1},{6,2},{7,3},{8,4},{9,5},{1... | collective-permute-start | bytes 2359304 | tf_op jit(solution)/shard_map/ppermute | solution.py:24
  55.7 19.8 %collective-permute-start.5 = (bf16[512,768]{1,0:T(8,128)(2,1)}, bf16[512,768]{1,0:T(8,128)(2,1)}, u32[]{:S(2)}, u32[]{:S(2)}) collective-permute-start(bf16[512,768]{1,0:T(8,128)(2,1)} %collective-permute-done.4.refs_8_), channel_id=1, source_target_pairs={{0,4},{1,5},{2,6},{3,7},{4,8},{5,9},{6,10},{7,11},{8,12},{9,13},{1... | collective-permute-start | bytes 2359304 | tf_op jit(solution)/shard_map/ppermute | solution.py:24
  55.8 25.2 %collective-permute-start.2 = (bf16[128,4096]{1,0:T(8,128)(2,1)S(1)}, bf16[128,4096]{1,0:T(8,128)(2,1)}, u32[]{:S(2)}, u32[]{:S(2)}) collective-permute-start(bf16[128,4096]{1,0:T(8,128)(2,1)S(1)} %collective-permute-done.1.refs_2_), channel_id=1, source_target_pairs={{0,1},{1,0},{2,3},{3,2},{4,5},{5,4},{6,7},{7,6},{8,9},{9,8},{10,11... | collective-permute-start | bytes 3145736 | tf_op jit(solution)/shard_map/ppermute | solution.py:19
  75.4 21.4 %collective-permute-start.13 = (bf16[128,4096]{1,0:T(8,128)(2,1)}, bf16[128,4096]{1,0:T(8,128)(2,1)S(1)}, u32[]{:S(2)}, u32[]{:S(2)}) collective-permute-start(bf16[128,4096]{1,0:T(8,128)(2,1)} %collective-permute-done.12.refs_0_), channel_id=1, source_target_pairs={{0,1},{1,0},{2,3},{3,2},{4,5},{5,4},{6,7},{7,6},{8,9},{9,8},{10,11... | collective-permute-start | bytes 3145736 | tf_op jit(solution)/shard_map/ppermute | solution.py:19
  75.5 15.8 %collective-permute-start.11 = (bf16[512,512]{1,0:T(8,128)(2,1)}, bf16[512,512]{1,0:T(8,128)(2,1)S(1)}, u32[]{:S(2)}, u32[]{:S(2)}) collective-permute-start(bf16[512,512]{1,0:T(8,128)(2,1)} %copy-done), channel_id=1, source_target_pairs={{0,4},{1,5},{2,6},{3,7},{4,8},{5,9},{6,10},{7,11},{8,12},{9,13},{1... | collective-permute-start | bytes 1572872 | tf_op jit(solution)/shard_map/ppermute | solution.py:24
  75.6 21.3 %collective-permute-start.9 = (bf16[512,512]{1,0:T(8,128)(2,1)}, bf16[512,512]{1,0:T(8,128)(2,1)S(1)}, u32[]{:S(2)}, u32[]{:S(2)}) collective-permute-start(bf16[512,512]{1,0:T(8,128)(2,1)} %copy-done.3), channel_id=1, source_target_pairs={{0,12},{1,13},{2,14},{3,15},{4,0},{5,1},{6,2},{7,3},{8,4},{9,5},{1... | collective-permute-start | bytes 1572872 | tf_op jit(solution)/shard_map/ppermute | solution.py:24
  100.7 12.4 %collective-permute-start.18 = (bf16[256,256]{1,0:T(8,128)(2,1)S(1)}, bf16[256,256]{1,0:T(8,128)(2,1)S(1)}, u32[]{:S(2)}, u32[]{:S(2)}) collective-permute-start(bf16[256,256]{1,0:T(8,128)(2,1)S(1)} %get-tuple-element.25.kl_ref), channel_id=1, source_target_pairs={{0,4},{1,5},{2,6},{3,7},{4,8},{5,9},{6,10},{7,11},{8,12},{9,13},{1... | collective-permute-start | bytes 393224 | tf_op jit(solution)/shard_map/ppermute | solution.py:28
  102.0 19.9 %collective-permute-start.20 = (bf16[256,256]{1,0:T(8,128)(2,1)S(1)}, bf16[256,256]{1,0:T(8,128)(2,1)S(1)}, u32[]{:S(2)}, u32[]{:S(2)}) collective-permute-start(bf16[256,256]{1,0:T(8,128)(2,1)S(1)} %get-tuple-element.25.kl_ref), channel_id=1, source_target_pairs={{0,8},{1,9},{2,10},{3,11},{4,12},{5,13},{6,14},{7,15},{16,24},{17,... | collective-permute-start | bytes 393224 | tf_op jit(solution)/shard_map/ppermute | solution.py:28
  105.6 16.3 %collective-permute-start.22 = (bf16[256,256]{1,0:T(8,128)(2,1)S(1)}, bf16[256,256]{1,0:T(8,128)(2,1)S(1)}, u32[]{:S(2)}, u32[]{:S(2)}) collective-permute-start(bf16[256,256]{1,0:T(8,128)(2,1)S(1)} %get-tuple-element.25.kl_ref), channel_id=1, source_target_pairs={{0,12},{1,13},{2,14},{3,15},{16,28},{17,29},{18,30},{19,31},{32,44... | collective-permute-start | bytes 393224 | tf_op jit(solution)/shard_map/ppermute | solution.py:28
  106.9 15.0 %collective-permute-start.17 = (bf16[768,256]{1,0:T(8,128)(2,1)S(1)}, bf16[768,256]{1,0:T(8,128)(2,1)S(1)}, u32[]{:S(2)}, u32[]{:S(2)}) collective-permute-start(bf16[768,256]{1,0:T(8,128)(2,1)S(1)} %get-tuple-element.24.ke_ref), channel_id=1, source_target_pairs={{0,4},{1,5},{2,6},{3,7},{4,8},{5,9},{6,10},{7,11},{8,12},{9,13},{1... | collective-permute-start | bytes 1179656 | tf_op jit(solution)/shard_map/ppermute | solution.py:28
  108.3 16.7 %collective-permute-start.19 = (bf16[768,256]{1,0:T(8,128)(2,1)S(1)}, bf16[768,256]{1,0:T(8,128)(2,1)S(1)}, u32[]{:S(2)}, u32[]{:S(2)}) collective-permute-start(bf16[768,256]{1,0:T(8,128)(2,1)S(1)} %get-tuple-element.24.ke_ref), channel_id=1, source_target_pairs={{0,8},{1,9},{2,10},{3,11},{4,12},{5,13},{6,14},{7,15},{16,24},{17,... | collective-permute-start | bytes 1179656 | tf_op jit(solution)/shard_map/ppermute | solution.py:28
  113.1 13.0 %collective-permute-start.21 = (bf16[768,256]{1,0:T(8,128)(2,1)S(1)}, bf16[768,256]{1,0:T(8,128)(2,1)S(1)}, u32[]{:S(2)}, u32[]{:S(2)}) collective-permute-start(bf16[768,256]{1,0:T(8,128)(2,1)S(1)} %get-tuple-element.24.ke_ref), channel_id=1, source_target_pairs={{0,12},{1,13},{2,14},{3,15},{16,28},{17,29},{18,30},{19,31},{32,44... | collective-permute-start | bytes 1179656 | tf_op jit(solution)/shard_map/ppermute | solution.py:28
  131.0 30.9 %collective-permute-start.26 = (bf16[256,512]{1,0:T(8,128)(2,1)S(1)}, bf16[256,512]{1,0:T(8,128)(2,1)S(1)}, u32[]{:S(2)}, u32[]{:S(2)}) collective-permute-start(bf16[256,512]{1,0:T(8,128)(2,1)S(1)} %shard_map.64), channel_id=1, source_target_pairs={{0,19},{1,18},{2,17},{3,16},{4,23},{5,22},{6,21},{7,20},{8,27},{9,... | collective-permute-start | bytes 786440 | tf_op jit(solution)/shard_map/ppermute | solution.py:35
  137.0 19.3 %collective-permute-start.24 = (bf16[256,512]{1,0:T(8,128)(2,1)S(1)}, bf16[256,512]{1,0:T(8,128)(2,1)S(1)}, u32[]{:S(2)}, u32[]{:S(2)}) collective-permute-start(bf16[256,512]{1,0:T(8,128)(2,1)S(1)} %shard_map.62), channel_id=1, source_target_pairs={{0,17},{1,16},{2,19},{3,18},{4,21},{5,20},{6,23},{7,22},{8,25},{9,... | collective-permute-start | bytes 786440 | tf_op jit(solution)/shard_map/ppermute | solution.py:35
  145.2 11.1 %collective-permute-start.23 = (bf16[256,512]{1,0:T(8,128)(2,1)S(1)}, bf16[256,512]{1,0:T(8,128)(2,1)S(1)}, u32[]{:S(2)}, u32[]{:S(2)}) collective-permute-start(bf16[256,512]{1,0:T(8,128)(2,1)S(1)} %shard_map.61), channel_id=1, source_target_pairs={{0,16},{1,17},{2,18},{3,19},{4,20},{5,21},{6,22},{7,23},{8,24},{9,... | collective-permute-start | bytes 786440 | tf_op jit(solution)/shard_map/ppermute | solution.py:35
  (18 other events, 126.7 us)

commit v3 on v2

--- a/solution.py
+++ b/solution.py
@@ -319,29 +319,40 @@
         kv = refs[: len(flat)]
         out_ref, s_ref = refs[len(flat) :]
         z = place_ref[0]
-        first_row = piece * rows
-        stacked = jnp.concatenate(
-            [q_ref[first_row : first_row + rows, h * HEAD : (h + 1) * HEAD] for h in range(heads)], axis=0
-        )
-        key_scores(s_ref, stacked, kv)
-        v = values_and_ones(kv)
-        for h in range(heads):
-            mine = slice(h * rows, (h + 1) * rows)
-            old = tops_ref[piece, :, h * HEAD : (h + 1) * HEAD]
-            found, top, at = [], old, 0
-            for d, slab in enumerate(below, start=1):
-                n = sum(p.shape[0] for p in slab)
-                s = s_ref[mine, at : at + n]
-                at += n
-                found.append((s, z >= d))
-                top = jnp.maximum(top, jnp.where(z >= d, best_of(s), NEG))
-            top = jnp.max(top, axis=1, keepdims=True)
-            mixed = weigh([(s, jnp.where(visible, top, -NEG)) for s, visible in found], v)
-            shrink = jnp.exp2((old - top) * LOG2E_SCALE)
-            at = 2 * h * HEAD
-            above = mixed[:, :HEAD] + sums_ref[piece, :, at : at + HEAD] * shrink
-            under = mixed[:, HEAD:] + sums_ref[piece, :, at + HEAD : at + 2 * HEAD] * shrink
-            out_ref[:, h * HEAD : (h + 1) * HEAD] = (above / under).astype(jnp.bfloat16)
+
+        def lowest():
+            for h in range(heads):
+                at = 2 * h * HEAD
+                own = sums_ref[piece, :, at : at + 2 * HEAD]
+                out_ref[:, h * HEAD : (h + 1) * HEAD] = (own[:, :HEAD] / own[:, HEAD:]).astype(jnp.bfloat16)
+
+        def merged():
+            first_row = piece * rows
+            stacked = jnp.concatenate(
+                [q_ref[first_row : first_row + rows, h * HEAD : (h + 1) * HEAD] for h in range(heads)], axis=0
+            )
+            key_scores(s_ref, stacked, kv)
+            v = values_and_ones(kv)
+            for h in range(heads):
+                mine = slice(h * rows, (h + 1) * rows)
+                old = tops_ref[piece, :, h * HEAD : (h + 1) * HEAD]
+                found, top, at = [], old, 0
+                for d, slab in enumerate(below, start=1):
+                    n = sum(p.shape[0] for p in slab)
+                    s = s_ref[mine, at : at + n]
+                    at += n
+                    found.append((s, z >= d))
+                    top = jnp.maximum(top, jnp.where(z >= d, best_of(s), NEG))
+                top = jnp.max(top, axis=1, keepdims=True)
+                mixed = weigh([(s, jnp.where(visible, top, -NEG)) for s, visible in found], v)
+                shrink = jnp.exp2((old - top) * LOG2E_SCALE)
+                at = 2 * h * HEAD
+                above = mixed[:, :HEAD] + sums_ref[piece, :, at : at + HEAD] * shrink
+                under = mixed[:, HEAD:] + sums_ref[piece, :, at + HEAD : at + 2 * HEAD] * shrink
+                out_ref[:, h * HEAD : (h + 1) * HEAD] = (above / under).astype(jnp.bfloat16)
+
+        pl.when(z == 0)(lowest)
+        pl.when(z > 0)(merged)
 
     vmem = pl.BlockSpec(memory_space=pltpu.VMEM)
     return pl.pallas_call(
@@ -410,7 +421,7 @@
 
     sums, tops, queries = attend_own(place, q_early, q_late, kv_early, kv_late, early + late)
     out = jnp.zeros((rows, GROUP * GROUP * HEAD), jnp.bfloat16)
-    for k in range(GROUP):
+    for k in (0, 1, 3, 2):
         mixed = attend_below(place, sums, tops, queries, below, k)
         arrived = onward(mixed, k)
         out = lax.dynamic_update_slice(out, arrived, (0, (g ^ k) * GROUP * HEAD))

time: 164 us -> 164 us (level)
  the two profiles are of different devices: /device:TPU:0 before, /device:TPU:97 now
where the time goes in v3:
time: 164 us
  waiting for transfers between devices  72.1 us (44%)
  Pallas kernels  48.2 us (29%)
  starting transfers between devices  31.5 us (19%)
  local copies, waits for them, and re-layouts  8.48 us (5%)
  other arithmetic  3.22 us (2%)
    ppermute x8, waiting for transfers between devices, near(): lax.ppermute(block, 'seq', [(r, r ^ bits) for r in range(RING * GROUP)])  32.6 us
    pallas_call x4, Pallas kernels, attend_below(): pl.pallas_call(kernel, in_specs=[pl.BlockSpec(memory_space=pltpu.SMEM)] +...  20.4 us
    ppermute x9, waiting for transfers between devices, along(): lax.ppermute(block, 'seq', [(r, (r + step * GROUP) % n) for r in range(n)])  19.3 us
    ppermute x4, waiting for transfers between devices, onward(): return lax.ppermute(block, ('section', 'seq'), route)  10.4 us
    ppermute x6, waiting for transfers between devices, upward(): lax.ppermute(block, 'seq', [(a * GROUP + g, b * GROUP + g) for a, b in ro...  9.91 us
    ppermute x8, starting transfers between devices, near(): lax.ppermute(block, 'seq', [(r, r ^ bits) for r in range(RING * GROUP)])  8.57 us
    ppermute x9, starting transfers between devices, along(): lax.ppermute(block, 'seq', [(r, (r + step * GROUP) % n) for r in range(n)])  8.47 us
    ppermute x6, starting transfers between devices, upward(): lax.ppermute(block, 'seq', [(a * GROUP + g, b * GROUP + g) for a, b in ro...  7.75 us
  transfers between devices with their start and end apart: 27, of which 11 were waited for; matrix products, arithmetic and copies ran while one was open for 2% of the time, Pallas kernels for 24%

profile of v3, /device:TPU:97, one launch (start us, length us, event | category | flops | bytes accessed | tf_op | source)
XLA Modules:
  0.0 163.9 jit_solution(9808318268681678342)
XLA Ops:
  4.2 7.4 %collective-permute-done.6 = bf16[256,768]{1,0:T(8,128)(2,1)S(1)} collective-permute-done((bf16[256,768]{1,0:T(8,128)(2,1)S(1)}, bf16[256,768]{1,0:T(8,128)(2,1)S(1)}, u32[]{:S(2)}, u32[]{:S(2)}) %collective-permute-start.6) | collective-permute-done | bytes 393248 | tf_op jit(solution)/shard_map/ppermute | solution.py:19
  11.6 9.3 %collective-permute-done.7 = bf16[256,768]{1,0:T(8,128)(2,1)S(1)} collective-permute-done((bf16[256,768]{1,0:T(8,128)(2,1)S(1)}, bf16[256,768]{1,0:T(8,128)(2,1)S(1)}, u32[]{:S(2)}, u32[]{:S(2)}) %collective-permute-start.7) | collective-permute-done | bytes 393248 | tf_op jit(solution)/shard_map/ppermute | solution.py:19
  21.1 2.9 %shard_map.55 = (bf16[256,4096]{1,0:T(8,128)(2,1)S(1)}, bf16[128,4096]{1,0:T(8,128)(2,1)}, bf16[128,4096]{1,0:T(8,128)(2,1)}) custom-call(bf16[256,4096]{1,0:T(8,128)(2,1)S(1)} %bitcast.35, bf16[1,4096]{1,0:T(2,128)(2,1)S(1)} %copy-done.11), custom_call_target="tpu_custom_call" | custom-call | flops 4194304 | bytes 6291456 | tf_op jit(solution)/shard_map/pallas_call | solution.py:58
  25.4 2.6 %collective-permute-start.15 = (bf16[512,256]{1,0:T(8,128)(2,1)S(1)}, bf16[512,256]{1,0:T(8,128)(2,1)S(1)}, u32[]{:S(2)}, u32[]{:S(2)}) collective-permute-start(bf16[512,256]{1,0:T(8,128)(2,1)S(1)} %pad_maximum_fusion.5.refs_5_), channel_id=1, source_target_pairs={{0,4},{1,5},{2,6},{3,7},{4,8},{5,9},{6,10},{7,11},{8,12},{9,13},{1... | collective-permute-start | bytes 786440 | tf_op jit(solution)/shard_map/ppermute | solution.py:24
  30.5 2.7 %collective-permute-done.15.refs_9_ = bf16[512,256]{1,0:T(8,128)(2,1)S(1)} collective-permute-done((bf16[512,256]{1,0:T(8,128)(2,1)S(1)}, bf16[512,256]{1,0:T(8,128)(2,1)S(1)}, u32[]{:S(2)}, u32[]{:S(2)}) %collective-permute-start.15) | collective-permute-done | bytes 262176 | tf_op jit(solution)/shard_map/ppermute | solution.py:24
  33.9 4.8 %collective-permute-done.16.refs_11_ = bf16[512,256]{1,0:T(8,128)(2,1)S(1)} collective-permute-done((bf16[512,256]{1,0:T(8,128)(2,1)S(1)}, bf16[512,256]{1,0:T(8,128)(2,1)S(1)}, u32[]{:S(2)}, u32[]{:S(2)}) %collective-permute-start.16) | collective-permute-done | bytes 262176 | tf_op jit(solution)/shard_map/ppermute | solution.py:24
  41.2 8.8 %collective-permute-done.8.refs_7_ = bf16[512,512]{1,0:T(8,128)(2,1)S(1)} collective-permute-done((bf16[512,512]{1,0:T(8,128)(2,1)S(1)}, bf16[512,512]{1,0:T(8,128)(2,1)S(1)}, u32[]{:S(2)}, u32[]{:S(2)}) %collective-permute-start.8) | collective-permute-done | bytes 524320 | tf_op jit(solution)/shard_map/ppermute | solution.py:24
  50.8 2.8 %collective-permute-start.5 = (bf16[512,768]{1,0:T(8,128)(2,1)}, bf16[512,768]{1,0:T(8,128)(2,1)}, u32[]{:S(2)}, u32[]{:S(2)}) collective-permute-start(bf16[512,768]{1,0:T(8,128)(2,1)} %collective-permute-done.4.refs_8_), channel_id=1, source_target_pairs={{0,4},{1,5},{2,6},{3,7},{4,8},{5,9},{6,10},{7,11},{8,12},{9,13},{1... | collective-permute-start | bytes 2359304 | tf_op jit(solution)/shard_map/ppermute | solution.py:24
  55.5 15.9 %collective-permute-done.12.refs_0_ = bf16[128,4096]{1,0:T(8,128)(2,1)} collective-permute-done((bf16[128,4096]{1,0:T(8,128)(2,1)}, bf16[128,4096]{1,0:T(8,128)(2,1)}, u32[]{:S(2)}, u32[]{:S(2)}) %collective-permute-start.12) | collective-permute-done | bytes 1048608 | tf_op jit(solution)/shard_map/ppermute | solution.py:19
  72.4 2.6 %collective-permute-start.11 = (bf16[512,512]{1,0:T(8,128)(2,1)}, bf16[512,512]{1,0:T(8,128)(2,1)S(1)}, u32[]{:S(2)}, u32[]{:S(2)}) collective-permute-start(bf16[512,512]{1,0:T(8,128)(2,1)} %copy-done), channel_id=1, source_target_pairs={{0,4},{1,5},{2,6},{3,7},{4,8},{5,9},{6,10},{7,11},{8,12},{9,13},{1... | collective-permute-start | bytes 1572872 | tf_op jit(solution)/shard_map/ppermute | solution.py:24
  80.1 4.8 %shard_map.58 = (bf16[768,256]{1,0:T(8,128)(2,1)S(1)}, bf16[4096,256]{1,0:T(8,128)(2,1)S(1)}) custom-call(s32[2]{0:T(128)S(1)} %pad_add_fusion.place_ref, bf16[256,4096]{1,0:T(8,128)(2,1)S(1)} %get-tuple-element.17.refs_0_, bf16[256,4096]{1,0:T(8,128)(2,1)} %collective-permute-done.refs_1_, bf16[128,4096]{1,0:T(8,128)(2,1)S(1)} %collective-permute-done.1.refs_2_, ...), custom_call_target="tpu_custom_call" | custom-call | flops 1610612736 | bytes 8388608 | tf_op jit(solution)/shard_map/pallas_call | solution.py:147
  86.6 5.6 %shard_map.56 = (f32[768,512]{1,0:T(8,128)S(1)}, bf16[3072,512]{1,0:T(8,128)(2,1)S(1)}) custom-call(s32[2]{0:T(128)S(1)} %pad_add_fusion.place_ref, bf16[256,4096]{1,0:T(8,128)(2,1)S(1)} %get-tuple-element.17.refs_0_, bf16[256,4096]{1,0:T(8,128)(2,1)} %collective-permute-done.refs_1_, bf16[128,4096]{1,0:T(8,128)(2,1)S(1)} %collective-permute-done.1.refs_2_, ...), custom_call_target="tpu_custom_call" | custom-call | flops 2415919104 | bytes 7864320 | tf_op jit(solution)/shard_map/pallas_call | solution.py:174
  92.2 3.8 %shard_map.59 = (bf16[256,256]{1,0:T(8,128)(2,1)S(1)}, bf16[256,512]{1,0:T(8,128)(2,1)S(1)}) custom-call(s32[2]{0:T(128)S(1)} %pad_add_fusion.place_ref, bf16[128,4096]{1,0:T(8,128)(2,1)} %collective-permute-done.12.refs_0_, bf16[128,4096]{1,0:T(8,128)(2,1)S(1)} %collective-permute-done.13.refs_1_, bf16[4096,256]{1,0:T(8,128)(2,1)S(1)} %get-tuple-element.21.refs_2_, ...), custom_call_target="tpu_custom_call" | custom-call | flops 1610612736 | bytes 8388608 | tf_op jit(solution)/shard_map/pallas_call | solution.py:226
  102.5 3.5 %shard_map.57.qe_ref = bf16[768,512]{1,0:T(8,128)(2,1)S(1)} custom-call(s32[2]{0:T(128)S(1)} %pad_add_fusion.place_ref, bf16[256,4096]{1,0:T(8,128)(2,1)S(1)} %get-tuple-element.17.refs_0_, bf16[256,4096]{1,0:T(8,128)(2,1)} %collective-permute-done.refs_1_, bf16[128,4096]{1,0:T(8,128)(2,1)S(1)} %collective-permute-done.1.refs_2_, ...), custom_call_target="tpu_custom_call" | custom-call | flops 805306368 | bytes 2621440 | tf_op jit(solution)/shard_map/pallas_call | solution.py:196
  107.3 7.3 %shard_map.60 = (f32[4,256,1024]{2,1,0:T(8,128)S(1)}, f32[4,256,512]{2,1,0:T(8,128)S(1)}, bf16[1024,512]{1,0:T(8,128)(2,1)S(1)}) custom-call(s32[2]{0:T(128)S(1)} %pad_add_fusion.place_ref, bf16[768,512]{1,0:T(8,128)(2,1)S(1)} %shard_map.57.qe_ref, bf16[256,512]{1,0:T(8,128)(2,1)S(1)} %get-tuple-element.23.ql_ref, ...), custom_call_target="tpu_custom_call" | custom-call | flops 4294967296 | bytes 3145728 | tf_op jit(solution)/shard_map/pallas_call | solution.py:294
  114.6 9.9 %collective-permute-done.21.refs_4_ = bf16[768,256]{1,0:T(8,128)(2,1)S(1)} collective-permute-done((bf16[768,256]{1,0:T(8,128)(2,1)S(1)}, bf16[768,256]{1,0:T(8,128)(2,1)S(1)}, u32[]{:S(2)}, u32[]{:S(2)}) %collective-permute-start.21) | collective-permute-done | bytes 393248 | tf_op jit(solution)/shard_map/ppermute | solution.py:28
  124.5 5.2 %shard_map.64 = bf16[256,512]{1,0:T(8,128)(2,1)S(1)} custom-call(s32[2]{0:T(128)S(1)} %pad_add_fusion.place_ref, f32[4,256,1024]{2,1,0:T(8,128)S(1)} %get-tuple-element.26.sums_ref, f32[4,256,512]{2,1,0:T(8,128)S(1)} %get-tuple-element.27.tops_ref, bf16[1024,512]{1,0:T(8,128)(2,1)S(1)} %get-tuple-element.28.q_ref, ...), custom_call_target="tpu_custom_call" | custom-call | flops 3221225472 | bytes 3145728 | tf_op jit(solution)/shard_map/pallas_call | solution.py:358
  129.7 2.3 %collective-permute-start.26 = (bf16[256,512]{1,0:T(8,128)(2,1)S(1)}, bf16[256,512]{1,0:T(8,128)(2,1)S(1)}, u32[]{:S(2)}, u32[]{:S(2)}) collective-permute-start(bf16[256,512]{1,0:T(8,128)(2,1)S(1)} %shard_map.64), channel_id=1, source_target_pairs={{0,18},{1,19},{2,16},{3,17},{4,22},{5,23},{6,20},{7,21},{8,26},{9,... | collective-permute-start | bytes 786440 | tf_op jit(solution)/shard_map/ppermute | solution.py:35
  132.0 5.0 %shard_map.62 = bf16[256,512]{1,0:T(8,128)(2,1)S(1)} custom-call(s32[2]{0:T(128)S(1)} %pad_add_fusion.place_ref, f32[4,256,1024]{2,1,0:T(8,128)S(1)} %get-tuple-element.26.sums_ref, f32[4,256,512]{2,1,0:T(8,128)S(1)} %get-tuple-element.27.tops_ref, bf16[1024,512]{1,0:T(8,128)(2,1)S(1)} %get-tuple-element.28.q_ref, ...), custom_call_target="tpu_custom_call" | custom-call | flops 3221225472 | bytes 3145728 | tf_op jit(solution)/shard_map/pallas_call | solution.py:358
  137.0 3.2 %collective-permute-start.24 = (bf16[256,512]{1,0:T(8,128)(2,1)S(1)}, bf16[256,512]{1,0:T(8,128)(2,1)S(1)}, u32[]{:S(2)}, u32[]{:S(2)}) collective-permute-start(bf16[256,512]{1,0:T(8,128)(2,1)S(1)} %shard_map.62), channel_id=1, source_target_pairs={{0,17},{1,16},{2,19},{3,18},{4,21},{5,20},{6,23},{7,22},{8,25},{9,... | collective-permute-start | bytes 786440 | tf_op jit(solution)/shard_map/ppermute | solution.py:35
  140.2 5.2 %shard_map.61 = bf16[256,512]{1,0:T(8,128)(2,1)S(1)} custom-call(s32[2]{0:T(128)S(1)} %pad_add_fusion.place_ref, f32[4,256,1024]{2,1,0:T(8,128)S(1)} %get-tuple-element.26.sums_ref, f32[4,256,512]{2,1,0:T(8,128)S(1)} %get-tuple-element.27.tops_ref, bf16[1024,512]{1,0:T(8,128)(2,1)S(1)} %get-tuple-element.28.q_ref, ...), custom_call_target="tpu_custom_call" | custom-call | flops 3221225472 | bytes 3145728 | tf_op jit(solution)/shard_map/pallas_call | solution.py:358
  146.4 5.0 %shard_map.63 = bf16[256,512]{1,0:T(8,128)(2,1)S(1)} custom-call(s32[2]{0:T(128)S(1)} %pad_add_fusion.place_ref, f32[4,256,1024]{2,1,0:T(8,128)S(1)} %get-tuple-element.26.sums_ref, f32[4,256,512]{2,1,0:T(8,128)S(1)} %get-tuple-element.27.tops_ref, bf16[1024,512]{1,0:T(8,128)(2,1)S(1)} %get-tuple-element.28.q_ref, ...), custom_call_target="tpu_custom_call" | custom-call | flops 3221225472 | bytes 3145728 | tf_op jit(solution)/shard_map/pallas_call | solution.py:358
  151.6 4.9 %collective-permute-done.23 = bf16[256,512]{1,0:T(8,128)(2,1)S(1)} collective-permute-done((bf16[256,512]{1,0:T(8,128)(2,1)S(1)}, bf16[256,512]{1,0:T(8,128)(2,1)S(1)}, u32[]{:S(2)}, u32[]{:S(2)}) %collective-permute-start.23) | collective-permute-done | bytes 262176 | tf_op jit(solution)/shard_map/ppermute | solution.py:35
  156.7 5.5 %collective-permute-done.25 = bf16[256,512]{1,0:T(8,128)(2,1)S(1)} collective-permute-done((bf16[256,512]{1,0:T(8,128)(2,1)S(1)}, bf16[256,512]{1,0:T(8,128)(2,1)S(1)}, u32[]{:S(2)}, u32[]{:S(2)}) %collective-permute-start.25) | collective-permute-done | bytes 262176 | tf_op jit(solution)/shard_map/ppermute | solution.py:35
  (99 shorter events, 32.8 us)
Async XLA Ops:
  1.5 10.1 %collective-permute-start.6 = (bf16[256,768]{1,0:T(8,128)(2,1)S(1)}, bf16[256,768]{1,0:T(8,128)(2,1)S(1)}, u32[]{:S(2)}, u32[]{:S(2)}) collective-permute-start(bf16[256,768]{1,0:T(8,128)(2,1)S(1)} %pad_maximum_fusion.3), channel_id=1, source_target_pairs={{0,2},{1,3},{2,0},{3,1},{4,6},{5,7},{6,4},{7,5},{8,10},{9,11},{10,... | collective-permute-start | bytes 1179656 | tf_op jit(solution)/shard_map/ppermute | solution.py:19
  2.9 17.9 %collective-permute-start.7 = (bf16[256,768]{1,0:T(8,128)(2,1)S(1)}, bf16[256,768]{1,0:T(8,128)(2,1)S(1)}, u32[]{:S(2)}, u32[]{:S(2)}) collective-permute-start(bf16[256,768]{1,0:T(8,128)(2,1)S(1)} %pad_maximum_fusion.4), channel_id=1, source_target_pairs={{0,3},{1,2},{2,1},{3,0},{4,7},{5,6},{6,5},{7,4},{8,11},{9,10},{10,... | collective-permute-start | bytes 1179656 | tf_op jit(solution)/shard_map/ppermute | solution.py:19
  4.1 23.9 %collective-permute-start.3 = (bf16[256,768]{1,0:T(8,128)(2,1)S(1)}, bf16[256,768]{1,0:T(8,128)(2,1)S(1)}, u32[]{:S(2)}, u32[]{:S(2)}) collective-permute-start(bf16[256,768]{1,0:T(8,128)(2,1)S(1)} %pad_maximum_fusion.2), channel_id=1, source_target_pairs={{0,1},{1,0},{2,3},{3,2},{4,5},{5,4},{6,7},{7,6},{8,9},{9,8},{10,11... | collective-permute-start | bytes 1179656 | tf_op jit(solution)/shard_map/ppermute | solution.py:19
  24.0 29.6 %collective-permute-start.1 = (bf16[128,4096]{1,0:T(8,128)(2,1)}, bf16[128,4096]{1,0:T(8,128)(2,1)S(1)}, u32[]{:S(2)}, u32[]{:S(2)}) collective-permute-start(bf16[128,4096]{1,0:T(8,128)(2,1)} %get-tuple-element.18), channel_id=1, source_target_pairs={{0,2},{1,3},{2,0},{3,1},{4,6},{5,7},{6,4},{7,5},{8,10},{9,11},{10,... | collective-permute-start | bytes 3145736 | tf_op jit(solution)/shard_map/ppermute | solution.py:19
  25.3 52.0 %collective-permute-start = (bf16[256,4096]{1,0:T(8,128)(2,1)S(1)}, bf16[256,4096]{1,0:T(8,128)(2,1)}, u32[]{:S(2)}, u32[]{:S(2)}) collective-permute-start(bf16[256,4096]{1,0:T(8,128)(2,1)S(1)} %get-tuple-element.17.refs_0_), channel_id=1, source_target_pairs={{0,1},{1,0},{2,3},{3,2},{4,5},{5,4},{6,7},{7,6},{8,9},{9,8},{10,11... | collective-permute-start | bytes 6291464 | tf_op jit(solution)/shard_map/ppermute | solution.py:19
  28.9 21.9 %collective-permute-start.4 = (bf16[512,768]{1,0:T(8,128)(2,1)}, bf16[512,768]{1,0:T(8,128)(2,1)}, u32[]{:S(2)}, u32[]{:S(2)}) collective-permute-start(bf16[512,768]{1,0:T(8,128)(2,1)} %pad_maximum_fusion.refs_4_), channel_id=1, source_target_pairs={{0,4},{1,5},{2,6},{3,7},{4,8},{5,9},{6,10},{7,11},{8,12},{9,13},{1... | collective-permute-start | bytes 2359304 | tf_op jit(solution)/shard_map/ppermute | solution.py:24
  33.9 16.0 %collective-permute-start.8 = (bf16[512,512]{1,0:T(8,128)(2,1)S(1)}, bf16[512,512]{1,0:T(8,128)(2,1)S(1)}, u32[]{:S(2)}, u32[]{:S(2)}) collective-permute-start(bf16[512,512]{1,0:T(8,128)(2,1)S(1)} %pad_maximum_fusion.1.refs_5_), channel_id=1, source_target_pairs={{0,12},{1,13},{2,14},{3,15},{4,0},{5,1},{6,2},{7,3},{8,4},{9,5},{1... | collective-permute-start | bytes 1572872 | tf_op jit(solution)/shard_map/ppermute | solution.py:24
  39.4 32.0 %collective-permute-start.12 = (bf16[128,4096]{1,0:T(8,128)(2,1)}, bf16[128,4096]{1,0:T(8,128)(2,1)}, u32[]{:S(2)}, u32[]{:S(2)}) collective-permute-start(bf16[128,4096]{1,0:T(8,128)(2,1)} %get-tuple-element.20), channel_id=1, source_target_pairs={{0,2},{1,3},{2,0},{3,1},{4,6},{5,7},{6,4},{7,5},{8,10},{9,11},{10,... | collective-permute-start | bytes 3145736 | tf_op jit(solution)/shard_map/ppermute | solution.py:19
  50.8 21.7 %collective-permute-start.10 = (bf16[512,768]{1,0:T(8,128)(2,1)}, bf16[512,768]{1,0:T(8,128)(2,1)}, u32[]{:S(2)}, u32[]{:S(2)}) collective-permute-start(bf16[512,768]{1,0:T(8,128)(2,1)} %pad_maximum_fusion.refs_4_), channel_id=1, source_target_pairs={{0,12},{1,13},{2,14},{3,15},{4,0},{5,1},{6,2},{7,3},{8,4},{9,5},{1... | collective-permute-start | bytes 2359304 | tf_op jit(solution)/shard_map/ppermute | solution.py:24
  50.8 24.2 %collective-permute-start.5 = (bf16[512,768]{1,0:T(8,128)(2,1)}, bf16[512,768]{1,0:T(8,128)(2,1)}, u32[]{:S(2)}, u32[]{:S(2)}) collective-permute-start(bf16[512,768]{1,0:T(8,128)(2,1)} %collective-permute-done.4.refs_8_), channel_id=1, source_target_pairs={{0,4},{1,5},{2,6},{3,7},{4,8},{5,9},{6,10},{7,11},{8,12},{9,13},{1... | collective-permute-start | bytes 2359304 | tf_op jit(solution)/shard_map/ppermute | solution.py:24
  53.6 23.7 %collective-permute-start.2 = (bf16[128,4096]{1,0:T(8,128)(2,1)S(1)}, bf16[128,4096]{1,0:T(8,128)(2,1)}, u32[]{:S(2)}, u32[]{:S(2)}) collective-permute-start(bf16[128,4096]{1,0:T(8,128)(2,1)S(1)} %collective-permute-done.1.refs_2_), channel_id=1, source_target_pairs={{0,1},{1,0},{2,3},{3,2},{4,5},{5,4},{6,7},{7,6},{8,9},{9,8},{10,11... | collective-permute-start | bytes 3145736 | tf_op jit(solution)/shard_map/ppermute | solution.py:19
  71.4 20.7 %collective-permute-start.13 = (bf16[128,4096]{1,0:T(8,128)(2,1)}, bf16[128,4096]{1,0:T(8,128)(2,1)S(1)}, u32[]{:S(2)}, u32[]{:S(2)}) collective-permute-start(bf16[128,4096]{1,0:T(8,128)(2,1)} %collective-permute-done.12.refs_0_), channel_id=1, source_target_pairs={{0,1},{1,0},{2,3},{3,2},{4,5},{5,4},{6,7},{7,6},{8,9},{9,8},{10,11... | collective-permute-start | bytes 3145736 | tf_op jit(solution)/shard_map/ppermute | solution.py:19
  72.4 14.2 %collective-permute-start.11 = (bf16[512,512]{1,0:T(8,128)(2,1)}, bf16[512,512]{1,0:T(8,128)(2,1)S(1)}, u32[]{:S(2)}, u32[]{:S(2)}) collective-permute-start(bf16[512,512]{1,0:T(8,128)(2,1)} %copy-done), channel_id=1, source_target_pairs={{0,4},{1,5},{2,6},{3,7},{4,8},{5,9},{6,10},{7,11},{8,12},{9,13},{1... | collective-permute-start | bytes 1572872 | tf_op jit(solution)/shard_map/ppermute | solution.py:24
  75.0 17.1 %collective-permute-start.9 = (bf16[512,512]{1,0:T(8,128)(2,1)}, bf16[512,512]{1,0:T(8,128)(2,1)S(1)}, u32[]{:S(2)}, u32[]{:S(2)}) collective-permute-start(bf16[512,512]{1,0:T(8,128)(2,1)} %copy-done.3), channel_id=1, source_target_pairs={{0,12},{1,13},{2,14},{3,15},{4,0},{5,1},{6,2},{7,3},{8,4},{9,5},{1... | collective-permute-start | bytes 1572872 | tf_op jit(solution)/shard_map/ppermute | solution.py:24
  96.0 10.0 %collective-permute-start.18 = (bf16[256,256]{1,0:T(8,128)(2,1)S(1)}, bf16[256,256]{1,0:T(8,128)(2,1)S(1)}, u32[]{:S(2)}, u32[]{:S(2)}) collective-permute-start(bf16[256,256]{1,0:T(8,128)(2,1)S(1)} %get-tuple-element.25.kl_ref), channel_id=1, source_target_pairs={{0,4},{1,5},{2,6},{3,7},{4,8},{5,9},{6,10},{7,11},{8,12},{9,13},{1... | collective-permute-start | bytes 393224 | tf_op jit(solution)/shard_map/ppermute | solution.py:28
  97.3 17.3 %collective-permute-start.20 = (bf16[256,256]{1,0:T(8,128)(2,1)S(1)}, bf16[256,256]{1,0:T(8,128)(2,1)S(1)}, u32[]{:S(2)}, u32[]{:S(2)}) collective-permute-start(bf16[256,256]{1,0:T(8,128)(2,1)S(1)} %get-tuple-element.25.kl_ref), channel_id=1, source_target_pairs={{0,8},{1,9},{2,10},{3,11},{4,12},{5,13},{6,14},{7,15},{16,24},{17,... | collective-permute-start | bytes 393224 | tf_op jit(solution)/shard_map/ppermute | solution.py:28
  98.6 16.0 %collective-permute-start.22 = (bf16[256,256]{1,0:T(8,128)(2,1)S(1)}, bf16[256,256]{1,0:T(8,128)(2,1)S(1)}, u32[]{:S(2)}, u32[]{:S(2)}) collective-permute-start(bf16[256,256]{1,0:T(8,128)(2,1)S(1)} %get-tuple-element.25.kl_ref), channel_id=1, source_target_pairs={{0,12},{1,13},{2,14},{3,15},{16,28},{17,29},{18,30},{19,31},{32,44... | collective-permute-start | bytes 393224 | tf_op jit(solution)/shard_map/ppermute | solution.py:28
  99.9 14.7 %collective-permute-start.17 = (bf16[768,256]{1,0:T(8,128)(2,1)S(1)}, bf16[768,256]{1,0:T(8,128)(2,1)S(1)}, u32[]{:S(2)}, u32[]{:S(2)}) collective-permute-start(bf16[768,256]{1,0:T(8,128)(2,1)S(1)} %get-tuple-element.24.ke_ref), channel_id=1, source_target_pairs={{0,4},{1,5},{2,6},{3,7},{4,8},{5,9},{6,10},{7,11},{8,12},{9,13},{1... | collective-permute-start | bytes 1179656 | tf_op jit(solution)/shard_map/ppermute | solution.py:28
  101.2 13.4 %collective-permute-start.19 = (bf16[768,256]{1,0:T(8,128)(2,1)S(1)}, bf16[768,256]{1,0:T(8,128)(2,1)S(1)}, u32[]{:S(2)}, u32[]{:S(2)}) collective-permute-start(bf16[768,256]{1,0:T(8,128)(2,1)S(1)} %get-tuple-element.24.ke_ref), channel_id=1, source_target_pairs={{0,8},{1,9},{2,10},{3,11},{4,12},{5,13},{6,14},{7,15},{16,24},{17,... | collective-permute-start | bytes 1179656 | tf_op jit(solution)/shard_map/ppermute | solution.py:28
  106.0 18.5 %collective-permute-start.21 = (bf16[768,256]{1,0:T(8,128)(2,1)S(1)}, bf16[768,256]{1,0:T(8,128)(2,1)S(1)}, u32[]{:S(2)}, u32[]{:S(2)}) collective-permute-start(bf16[768,256]{1,0:T(8,128)(2,1)S(1)} %get-tuple-element.24.ke_ref), channel_id=1, source_target_pairs={{0,12},{1,13},{2,14},{3,15},{16,28},{17,29},{18,30},{19,31},{32,44... | collective-permute-start | bytes 1179656 | tf_op jit(solution)/shard_map/ppermute | solution.py:28
  129.7 32.5 %collective-permute-start.26 = (bf16[256,512]{1,0:T(8,128)(2,1)S(1)}, bf16[256,512]{1,0:T(8,128)(2,1)S(1)}, u32[]{:S(2)}, u32[]{:S(2)}) collective-permute-start(bf16[256,512]{1,0:T(8,128)(2,1)S(1)} %shard_map.64), channel_id=1, source_target_pairs={{0,18},{1,19},{2,16},{3,17},{4,22},{5,23},{6,20},{7,21},{8,26},{9,... | collective-permute-start | bytes 786440 | tf_op jit(solution)/shard_map/ppermute | solution.py:35
  137.0 19.7 %collective-permute-start.24 = (bf16[256,512]{1,0:T(8,128)(2,1)S(1)}, bf16[256,512]{1,0:T(8,128)(2,1)S(1)}, u32[]{:S(2)}, u32[]{:S(2)}) collective-permute-start(bf16[256,512]{1,0:T(8,128)(2,1)S(1)} %shard_map.62), channel_id=1, source_target_pairs={{0,17},{1,16},{2,19},{3,18},{4,21},{5,20},{6,23},{7,22},{8,25},{9,... | collective-permute-start | bytes 786440 | tf_op jit(solution)/shard_map/ppermute | solution.py:35
  145.4 11.1 %collective-permute-start.23 = (bf16[256,512]{1,0:T(8,128)(2,1)S(1)}, bf16[256,512]{1,0:T(8,128)(2,1)S(1)}, u32[]{:S(2)}, u32[]{:S(2)}) collective-permute-start(bf16[256,512]{1,0:T(8,128)(2,1)S(1)} %shard_map.61), channel_id=1, source_target_pairs={{0,16},{1,17},{2,18},{3,19},{4,20},{5,21},{6,22},{7,23},{8,24},{9,... | collective-permute-start | bytes 786440 | tf_op jit(solution)/shard_map/ppermute | solution.py:35
  151.4 10.8 %collective-permute-start.25 = (bf16[256,512]{1,0:T(8,128)(2,1)S(1)}, bf16[256,512]{1,0:T(8,128)(2,1)S(1)}, u32[]{:S(2)}, u32[]{:S(2)}) collective-permute-start(bf16[256,512]{1,0:T(8,128)(2,1)S(1)} %shard_map.63), channel_id=1, source_target_pairs={{0,19},{1,18},{2,17},{3,16},{4,23},{5,22},{6,21},{7,20},{8,27},{9,... | collective-permute-start | bytes 786440 | tf_op jit(solution)/shard_map/ppermute | solution.py:35
  (18 other events, 109.0 us)
